TPU v7x, 16 devices: a whole 2x2x2 slice. The times are simulated.
16 devices in a mesh: data: 16 (over z, y, x, core).
Axes of the slice: x: 2, y: 2, z: 2, core: 2. Of those that a mesh axis runs over, the one named last changes fastest.
Arguments:
- feat_img: bfloat16 [16384, 1152], P('data')
- feat_txt: bfloat16 [16384, 1152], P('data')
- w_img: bfloat16 [1152, 1152], replicated
- w_txt: bfloat16 [1152, 1152], replicated
- log_temp: float32 [], replicated
- logit_bias: float32 [], replicated
- pair_ids: int32 [16384], P('data')
Outputs:
- output 1: float32 [], replicated
- output 2: float32 [], replicated
- output 3: float32 [], replicated
- output 4: float32 [1152, 1152], replicated
- output 5: float32 [1152, 1152], replicated
All inputs are finite; a program needn't handle non-finite values.
Results may differ from a plain program's by a relative error of at most 0.001.
Values are sent between devices in bfloat16 or wider.
A program may use at most 1 GiB of HBM per device.

v0:
```python
import jax
import jax.numpy as jnp
from jax import lax
from jax.sharding import PartitionSpec as P

CONTRACT_ROWS = (((0,), (0,)), ((), ()))
CONTRACT_COLS = (((1,), (1,)), ((), ()))


def embed_rows(feat_rows, weights):
    raw_emb = jnp.dot(feat_rows, weights, preferred_element_type=jnp.float32)
    inv_norm = lax.rsqrt(jnp.sum(raw_emb * raw_emb, axis=1, keepdims=True))
    unit_emb = raw_emb * inv_norm
    return unit_emb, inv_norm, unit_emb.astype(jnp.bfloat16)


def weight_grad(feat_rows, unit_emb, inv_norm, grad_emb):
    raw_grad = inv_norm * (grad_emb - unit_emb * jnp.sum(unit_emb * grad_emb, axis=1, keepdims=True))
    return lax.dot_general(feat_rows, raw_grad.astype(jnp.bfloat16), CONTRACT_ROWS, preferred_element_type=jnp.float32)


def tile_terms(emb_img, ids_img, emb_txt, ids_txt, temp_scale, logit_bias, total_rows):
    sim_tile = lax.dot_general(emb_img, emb_txt, CONTRACT_COLS, preferred_element_type=jnp.float32)
    label_sign = jnp.where(ids_img[:, None] == ids_txt[None, :], 1.0, -1.0).astype(jnp.float32)
    margin = -label_sign * (temp_scale * sim_tile + logit_bias)
    grad_tile = -label_sign * jax.nn.sigmoid(margin) / total_rows
    grad_bf = grad_tile.astype(jnp.bfloat16)
    part_img = jnp.dot(grad_bf, emb_txt, preferred_element_type=jnp.float32)
    part_txt = lax.dot_general(grad_bf, emb_img, CONTRACT_ROWS, preferred_element_type=jnp.float32)
    loss_part = jnp.sum(jax.nn.softplus(margin))
    return part_img, part_txt, loss_part, jnp.sum(grad_tile * sim_tile), jnp.sum(grad_tile)


def solution(mesh):
    n_dev = mesh.shape["data"]
    next_perm = [(src_dev, (src_dev + 1) % n_dev) for src_dev in range(n_dev)]

    def local_fn(feat_img, feat_txt, w_img, w_txt, log_temp, logit_bias, pair_ids):
        total_rows = feat_img.shape[0] * n_dev
        temp_scale = jnp.exp(log_temp)
        unit_img, inv_img, emb_img = embed_rows(feat_img, w_img)
        unit_txt, inv_txt, emb_txt = embed_rows(feat_txt, w_txt)

        def visit_block(hop_index, loop_state):
            txt_blk, ids_blk, acc_txt, acc_img, loss_sum, temp_sum, bias_sum = loop_state
            part_img, part_txt, loss_part, temp_part, bias_part = tile_terms(
                emb_img, pair_ids, txt_blk, ids_blk, temp_scale, logit_bias, total_rows)
            txt_blk, ids_blk, acc_txt = lax.ppermute((txt_blk, ids_blk, acc_txt + part_txt), "data", next_perm)
            return (txt_blk, ids_blk, acc_txt, acc_img + part_img,
                    loss_sum + loss_part, temp_sum + temp_part, bias_sum + bias_part)

        zero_rows = jnp.zeros(emb_img.shape, jnp.float32)
        zero_sum = jnp.zeros((), jnp.float32)
        loop_state = (emb_txt, pair_ids, zero_rows, zero_rows, zero_sum, zero_sum, zero_sum)
        loop_state = lax.fori_loop(0, n_dev - 1, visit_block, loop_state)
        txt_blk, ids_blk, acc_txt, acc_img, loss_sum, temp_sum, bias_sum = loop_state
        part_img, part_txt, loss_part, temp_part, bias_part = tile_terms(
            emb_img, pair_ids, txt_blk, ids_blk, temp_scale, logit_bias, total_rows)
        home_txt = lax.ppermute(acc_txt + part_txt, "data", next_perm)
        grad_img = temp_scale * (acc_img + part_img)
        grad_txt = temp_scale * home_txt
        dw_img = weight_grad(feat_img, unit_img, inv_img, grad_img)
        dw_txt = weight_grad(feat_txt, unit_txt, inv_txt, grad_txt)
        totals = lax.psum((loss_sum + loss_part, temp_sum + temp_part, bias_sum + bias_part, dw_img, dw_txt), "data")
        return totals[0] / total_rows, temp_scale * totals[1], totals[2], totals[3], totals[4]

    return jax.shard_map(
        local_fn,
        mesh=mesh,
        in_specs=(P("data", None), P("data", None), P(None, None), P(None, None), P(), P(), P("data")),
        out_specs=(P(), P(), P(), P(None, None), P(None, None)),
        check_vma=False,
    )
```

profile of v0, /device:TPU:0, one launch (start us, length us, event | category | flops | bytes accessed | tf_op | source)
XLA Modules:
  0.0 1813.2 jit_solution(11311605077620322538)
XLA Ops:
  31.4 1547.1 %while.23 = (s32[]{:T(128)}, bf16[1024,1152]{1,0:T(8,128)(2,1)S(1)}, s32[1024]{0:T(1024)S(1)}, f32[1024,1152]{1,0:T(8,128)}, f32[1024,1152]{1,0:T(8,128)}, /*ind...) while((s32[]{:T(128)}, ...), condition=%wide.region_6.7_spmd.clone, body=%wide.region_2.6_spmd.clone.sunk | while | flops 7298482176 | bytes 100188568 | solution.py:55
  68.7 67.0 %collective-permute-done.1 = s32[1024]{0:T(1024)S(1)} collective-permute-done((s32[1024]{0:T(1024)S(1)}, s32[1024]{0:T(1024)S(1)}, u32[]{:S(2)}, u32[]{:S(2)}) %collective-permute-start.1) | collective-permute-done | bytes 4128 | tf_op jit(solution)/shard_map/while/body/eval_jaxpr/ppermute | solution.py:48
  158.5 10.9 select_add_fusion.2
  171.3 67.4 %collective-permute-done.1 = s32[1024]{0:T(1024)S(1)} collective-permute-done((s32[1024]{0:T(1024)S(1)}, s32[1024]{0:T(1024)S(1)}, u32[]{:S(2)}, u32[]{:S(2)}) %collective-permute-start.1) | collective-permute-done | bytes 4128 | tf_op jit(solution)/shard_map/while/body/eval_jaxpr/ppermute | solution.py:48
  273.9 67.8 %collective-permute-done.1 = s32[1024]{0:T(1024)S(1)} collective-permute-done((s32[1024]{0:T(1024)S(1)}, s32[1024]{0:T(1024)S(1)}, u32[]{:S(2)}, u32[]{:S(2)}) %collective-permute-start.1) | collective-permute-done | bytes 4128 | tf_op jit(solution)/shard_map/while/body/eval_jaxpr/ppermute | solution.py:48
  364.2 10.9 select_add_fusion.2
  377.0 67.8 %collective-permute-done.1 = s32[1024]{0:T(1024)S(1)} collective-permute-done((s32[1024]{0:T(1024)S(1)}, s32[1024]{0:T(1024)S(1)}, u32[]{:S(2)}, u32[]{:S(2)}) %collective-permute-start.1) | collective-permute-done | bytes 4128 | tf_op jit(solution)/shard_map/while/body/eval_jaxpr/ppermute | solution.py:48
  467.2 10.9 select_add_fusion.2
  480.0 67.8 %collective-permute-done.1 = s32[1024]{0:T(1024)S(1)} collective-permute-done((s32[1024]{0:T(1024)S(1)}, s32[1024]{0:T(1024)S(1)}, u32[]{:S(2)}, u32[]{:S(2)}) %collective-permute-start.1) | collective-permute-done | bytes 4128 | tf_op jit(solution)/shard_map/while/body/eval_jaxpr/ppermute | solution.py:48
  570.3 10.9 select_add_fusion.2
  583.0 67.8 %collective-permute-done.1 = s32[1024]{0:T(1024)S(1)} collective-permute-done((s32[1024]{0:T(1024)S(1)}, s32[1024]{0:T(1024)S(1)}, u32[]{:S(2)}, u32[]{:S(2)}) %collective-permute-start.1) | collective-permute-done | bytes 4128 | tf_op jit(solution)/shard_map/while/body/eval_jaxpr/ppermute | solution.py:48
  673.3 10.9 select_add_fusion.2
  686.1 67.8 %collective-permute-done.1 = s32[1024]{0:T(1024)S(1)} collective-permute-done((s32[1024]{0:T(1024)S(1)}, s32[1024]{0:T(1024)S(1)}, u32[]{:S(2)}, u32[]{:S(2)}) %collective-permute-start.1) | collective-permute-done | bytes 4128 | tf_op jit(solution)/shard_map/while/body/eval_jaxpr/ppermute | solution.py:48
  776.4 10.9 select_add_fusion.2
  789.1 67.8 %collective-permute-done.1 = s32[1024]{0:T(1024)S(1)} collective-permute-done((s32[1024]{0:T(1024)S(1)}, s32[1024]{0:T(1024)S(1)}, u32[]{:S(2)}, u32[]{:S(2)}) %collective-permute-start.1) | collective-permute-done | bytes 4128 | tf_op jit(solution)/shard_map/while/body/eval_jaxpr/ppermute | solution.py:48
  879.4 10.9 select_add_fusion.2
  892.2 67.8 %collective-permute-done.1 = s32[1024]{0:T(1024)S(1)} collective-permute-done((s32[1024]{0:T(1024)S(1)}, s32[1024]{0:T(1024)S(1)}, u32[]{:S(2)}, u32[]{:S(2)}) %collective-permute-start.1) | collective-permute-done | bytes 4128 | tf_op jit(solution)/shard_map/while/body/eval_jaxpr/ppermute | solution.py:48
  982.4 10.9 select_add_fusion.2
  995.2 67.8 %collective-permute-done.1 = s32[1024]{0:T(1024)S(1)} collective-permute-done((s32[1024]{0:T(1024)S(1)}, s32[1024]{0:T(1024)S(1)}, u32[]{:S(2)}, u32[]{:S(2)}) %collective-permute-start.1) | collective-permute-done | bytes 4128 | tf_op jit(solution)/shard_map/while/body/eval_jaxpr/ppermute | solution.py:48
  1085.5 10.9 select_add_fusion.2
  1098.3 67.8 %collective-permute-done.1 = s32[1024]{0:T(1024)S(1)} collective-permute-done((s32[1024]{0:T(1024)S(1)}, s32[1024]{0:T(1024)S(1)}, u32[]{:S(2)}, u32[]{:S(2)}) %collective-permute-start.1) | collective-permute-done | bytes 4128 | tf_op jit(solution)/shard_map/while/body/eval_jaxpr/ppermute | solution.py:48
  1188.5 10.9 select_add_fusion.2
  1201.3 67.8 %collective-permute-done.1 = s32[1024]{0:T(1024)S(1)} collective-permute-done((s32[1024]{0:T(1024)S(1)}, s32[1024]{0:T(1024)S(1)}, u32[]{:S(2)}, u32[]{:S(2)}) %collective-permute-start.1) | collective-permute-done | bytes 4128 | tf_op jit(solution)/shard_map/while/body/eval_jaxpr/ppermute | solution.py:48
  1291.6 10.9 select_add_fusion.2
  1304.4 67.8 %collective-permute-done.1 = s32[1024]{0:T(1024)S(1)} collective-permute-done((s32[1024]{0:T(1024)S(1)}, s32[1024]{0:T(1024)S(1)}, u32[]{:S(2)}, u32[]{:S(2)}) %collective-permute-start.1) | collective-permute-done | bytes 4128 | tf_op jit(solution)/shard_map/while/body/eval_jaxpr/ppermute | solution.py:48
  1394.6 10.9 select_add_fusion.2
  1407.4 67.8 %collective-permute-done.1 = s32[1024]{0:T(1024)S(1)} collective-permute-done((s32[1024]{0:T(1024)S(1)}, s32[1024]{0:T(1024)S(1)}, u32[]{:S(2)}, u32[]{:S(2)}) %collective-permute-start.1) | collective-permute-done | bytes 4128 | tf_op jit(solution)/shard_map/while/body/eval_jaxpr/ppermute | solution.py:48
  1497.7 10.9 select_add_fusion.2
  1510.4 67.8 %collective-permute-done.1 = s32[1024]{0:T(1024)S(1)} collective-permute-done((s32[1024]{0:T(1024)S(1)}, s32[1024]{0:T(1024)S(1)}, u32[]{:S(2)}, u32[]{:S(2)}) %collective-permute-start.1) | collective-permute-done | bytes 4128 | tf_op jit(solution)/shard_map/while/body/eval_jaxpr/ppermute | solution.py:48
  1613.0 38.9 %collective-permute-done.3 = f32[1024,1152]{1,0:T(8,128)S(1)} collective-permute-done((f32[1024,1152]{1,0:T(8,128)S(1)}, f32[1024,1152]{1,0:T(8,128)S(1)}, u32[]{:S(2)}, u32[]{:S(2)}) %collective-permute-start.3) | collective-permute-done | bytes 4718624 | tf_op jit(solution)/shard_map/ppermute | solution.py:59
  1660.8 33.4 %all-reduce = (f32[]{:T(128)}, f32[]{:T(128)}, f32[]{:T(128)}) all-reduce(f32[]{:T(128)S(6)} %add.71, f32[]{:T(128)S(6)} %add.73, f32[]{:T(128)S(6)} %add.74), channel_id=1, replica_groups=mesh['data'=16] {'data'}, use_global_device_ids=true, to_apply=%region_8.9 | all-reduce | flops 3 | bytes 24 | tf_op jit(solution)/shard_map/psum | solution.py:64
  1695.5 94.3 %all-reduce.4.cloned.1.call-done = (f32[1152,1152]{0,1:T(8,128)}, f32[1152,1152]{0,1:T(8,128)}) async-done(((f32[1152,1152]{0,1:T(8,128)}, f32[1152,1152]{0,1:T(8,128)}), (f32[1152,1152]{0,1:T(8,128)}, f32[1152,1152]{0,1:T(8,128)})) %all-reduce.4.cloned.1.call-update) | async-done | bytes 10616848 | tf_op jit(solution)/shard_map/psum | solution.py:64
  (251 shorter events, 438.4 us)
Async XLA Ops:
  7.2 1782.6 %all-reduce.4.cloned.1.call-start = ((), (), s32[]{:S(2)}) async-start(), calls=%async_computation | async-start | bytes 21233664 | tf_op jit(solution)/shard_map/psum | solution.py:64
  53.9 81.8 %collective-permute-start.2 = (f32[1024,1152]{1,0:T(8,128)}, f32[1024,1152]{1,0:T(8,128)}, u32[]{:S(2)}, u32[]{:S(2)}) collective-permute-start(f32[1024,1152]{1,0:T(8,128)} %convolution_add_fusion.3), channel_id=1, source_target_pairs={{0,1},{1,2},{2,3},{3,4},{4,5},{5,6},{6,7},{7,8},{8,9},{9,10},{10,1... | collective-permute-start | bytes 14155784 | tf_op jit(solution)/shard_map/while/body/eval_jaxpr/ppermute | solution.py:48
  54.6 81.0 %collective-permute-start = (bf16[1024,1152]{1,0:T(8,128)(2,1)}, bf16[1024,1152]{1,0:T(8,128)(2,1)S(1)}, u32[]{:S(2)}, u32[]{:S(2)}) collective-permute-start(bf16[1024,1152]{1,0:T(8,128)(2,1)} %copy.23), channel_id=1, source_target_pairs={{0,1},{1,2},{2,3},{3,4},{4,5},{5,6},{6,7},{7,8},{8,9},{9,10},{10,1... | collective-permute-start | bytes 7077896 | tf_op jit(solution)/shard_map/while/body/eval_jaxpr/ppermute | solution.py:48
  158.0 80.7 %collective-permute-start.2 = (f32[1024,1152]{1,0:T(8,128)}, f32[1024,1152]{1,0:T(8,128)}, u32[]{:S(2)}, u32[]{:S(2)}) collective-permute-start(f32[1024,1152]{1,0:T(8,128)} %convolution_add_fusion.3), channel_id=1, source_target_pairs={{0,1},{1,2},{2,3},{3,4},{4,5},{5,6},{6,7},{7,8},{8,9},{9,10},{10,1... | collective-permute-start | bytes 14155784 | tf_op jit(solution)/shard_map/while/body/eval_jaxpr/ppermute | solution.py:48
  158.0 80.7 %collective-permute-start = (bf16[1024,1152]{1,0:T(8,128)(2,1)}, bf16[1024,1152]{1,0:T(8,128)(2,1)S(1)}, u32[]{:S(2)}, u32[]{:S(2)}) collective-permute-start(bf16[1024,1152]{1,0:T(8,128)(2,1)} %copy.23), channel_id=1, source_target_pairs={{0,1},{1,2},{2,3},{3,4},{4,5},{5,6},{6,7},{7,8},{8,9},{9,10},{10,1... | collective-permute-start | bytes 7077896 | tf_op jit(solution)/shard_map/while/body/eval_jaxpr/ppermute | solution.py:48
  261.1 80.7 %collective-permute-start.2 = (f32[1024,1152]{1,0:T(8,128)}, f32[1024,1152]{1,0:T(8,128)}, u32[]{:S(2)}, u32[]{:S(2)}) collective-permute-start(f32[1024,1152]{1,0:T(8,128)} %convolution_add_fusion.3), channel_id=1, source_target_pairs={{0,1},{1,2},{2,3},{3,4},{4,5},{5,6},{6,7},{7,8},{8,9},{9,10},{10,1... | collective-permute-start | bytes 14155784 | tf_op jit(solution)/shard_map/while/body/eval_jaxpr/ppermute | solution.py:48
  261.1 80.7 %collective-permute-start = (bf16[1024,1152]{1,0:T(8,128)(2,1)}, bf16[1024,1152]{1,0:T(8,128)(2,1)S(1)}, u32[]{:S(2)}, u32[]{:S(2)}) collective-permute-start(bf16[1024,1152]{1,0:T(8,128)(2,1)} %copy.23), channel_id=1, source_target_pairs={{0,1},{1,2},{2,3},{3,4},{4,5},{5,6},{6,7},{7,8},{8,9},{9,10},{10,1... | collective-permute-start | bytes 7077896 | tf_op jit(solution)/shard_map/while/body/eval_jaxpr/ppermute | solution.py:48
  364.1 80.7 %collective-permute-start.2 = (f32[1024,1152]{1,0:T(8,128)}, f32[1024,1152]{1,0:T(8,128)}, u32[]{:S(2)}, u32[]{:S(2)}) collective-permute-start(f32[1024,1152]{1,0:T(8,128)} %convolution_add_fusion.3), channel_id=1, source_target_pairs={{0,1},{1,2},{2,3},{3,4},{4,5},{5,6},{6,7},{7,8},{8,9},{9,10},{10,1... | collective-permute-start | bytes 14155784 | tf_op jit(solution)/shard_map/while/body/eval_jaxpr/ppermute | solution.py:48
  364.1 80.7 %collective-permute-start = (bf16[1024,1152]{1,0:T(8,128)(2,1)}, bf16[1024,1152]{1,0:T(8,128)(2,1)S(1)}, u32[]{:S(2)}, u32[]{:S(2)}) collective-permute-start(bf16[1024,1152]{1,0:T(8,128)(2,1)} %copy.23), channel_id=1, source_target_pairs={{0,1},{1,2},{2,3},{3,4},{4,5},{5,6},{6,7},{7,8},{8,9},{9,10},{10,1... | collective-permute-start | bytes 7077896 | tf_op jit(solution)/shard_map/while/body/eval_jaxpr/ppermute | solution.py:48
  467.2 80.7 %collective-permute-start.2 = (f32[1024,1152]{1,0:T(8,128)}, f32[1024,1152]{1,0:T(8,128)}, u32[]{:S(2)}, u32[]{:S(2)}) collective-permute-start(f32[1024,1152]{1,0:T(8,128)} %convolution_add_fusion.3), channel_id=1, source_target_pairs={{0,1},{1,2},{2,3},{3,4},{4,5},{5,6},{6,7},{7,8},{8,9},{9,10},{10,1... | collective-permute-start | bytes 14155784 | tf_op jit(solution)/shard_map/while/body/eval_jaxpr/ppermute | solution.py:48
  467.2 80.7 %collective-permute-start = (bf16[1024,1152]{1,0:T(8,128)(2,1)}, bf16[1024,1152]{1,0:T(8,128)(2,1)S(1)}, u32[]{:S(2)}, u32[]{:S(2)}) collective-permute-start(bf16[1024,1152]{1,0:T(8,128)(2,1)} %copy.23), channel_id=1, source_target_pairs={{0,1},{1,2},{2,3},{3,4},{4,5},{5,6},{6,7},{7,8},{8,9},{9,10},{10,1... | collective-permute-start | bytes 7077896 | tf_op jit(solution)/shard_map/while/body/eval_jaxpr/ppermute | solution.py:48
  570.2 80.7 %collective-permute-start.2 = (f32[1024,1152]{1,0:T(8,128)}, f32[1024,1152]{1,0:T(8,128)}, u32[]{:S(2)}, u32[]{:S(2)}) collective-permute-start(f32[1024,1152]{1,0:T(8,128)} %convolution_add_fusion.3), channel_id=1, source_target_pairs={{0,1},{1,2},{2,3},{3,4},{4,5},{5,6},{6,7},{7,8},{8,9},{9,10},{10,1... | collective-permute-start | bytes 14155784 | tf_op jit(solution)/shard_map/while/body/eval_jaxpr/ppermute | solution.py:48
  570.2 80.7 %collective-permute-start = (bf16[1024,1152]{1,0:T(8,128)(2,1)}, bf16[1024,1152]{1,0:T(8,128)(2,1)S(1)}, u32[]{:S(2)}, u32[]{:S(2)}) collective-permute-start(bf16[1024,1152]{1,0:T(8,128)(2,1)} %copy.23), channel_id=1, source_target_pairs={{0,1},{1,2},{2,3},{3,4},{4,5},{5,6},{6,7},{7,8},{8,9},{9,10},{10,1... | collective-permute-start | bytes 7077896 | tf_op jit(solution)/shard_map/while/body/eval_jaxpr/ppermute | solution.py:48
  673.2 80.7 %collective-permute-start.2 = (f32[1024,1152]{1,0:T(8,128)}, f32[1024,1152]{1,0:T(8,128)}, u32[]{:S(2)}, u32[]{:S(2)}) collective-permute-start(f32[1024,1152]{1,0:T(8,128)} %convolution_add_fusion.3), channel_id=1, source_target_pairs={{0,1},{1,2},{2,3},{3,4},{4,5},{5,6},{6,7},{7,8},{8,9},{9,10},{10,1... | collective-permute-start | bytes 14155784 | tf_op jit(solution)/shard_map/while/body/eval_jaxpr/ppermute | solution.py:48
  673.2 80.7 %collective-permute-start = (bf16[1024,1152]{1,0:T(8,128)(2,1)}, bf16[1024,1152]{1,0:T(8,128)(2,1)S(1)}, u32[]{:S(2)}, u32[]{:S(2)}) collective-permute-start(bf16[1024,1152]{1,0:T(8,128)(2,1)} %copy.23), channel_id=1, source_target_pairs={{0,1},{1,2},{2,3},{3,4},{4,5},{5,6},{6,7},{7,8},{8,9},{9,10},{10,1... | collective-permute-start | bytes 7077896 | tf_op jit(solution)/shard_map/while/body/eval_jaxpr/ppermute | solution.py:48
  776.3 80.7 %collective-permute-start.2 = (f32[1024,1152]{1,0:T(8,128)}, f32[1024,1152]{1,0:T(8,128)}, u32[]{:S(2)}, u32[]{:S(2)}) collective-permute-start(f32[1024,1152]{1,0:T(8,128)} %convolution_add_fusion.3), channel_id=1, source_target_pairs={{0,1},{1,2},{2,3},{3,4},{4,5},{5,6},{6,7},{7,8},{8,9},{9,10},{10,1... | collective-permute-start | bytes 14155784 | tf_op jit(solution)/shard_map/while/body/eval_jaxpr/ppermute | solution.py:48
  776.3 80.7 %collective-permute-start = (bf16[1024,1152]{1,0:T(8,128)(2,1)}, bf16[1024,1152]{1,0:T(8,128)(2,1)S(1)}, u32[]{:S(2)}, u32[]{:S(2)}) collective-permute-start(bf16[1024,1152]{1,0:T(8,128)(2,1)} %copy.23), channel_id=1, source_target_pairs={{0,1},{1,2},{2,3},{3,4},{4,5},{5,6},{6,7},{7,8},{8,9},{9,10},{10,1... | collective-permute-start | bytes 7077896 | tf_op jit(solution)/shard_map/while/body/eval_jaxpr/ppermute | solution.py:48
  879.3 80.7 %collective-permute-start.2 = (f32[1024,1152]{1,0:T(8,128)}, f32[1024,1152]{1,0:T(8,128)}, u32[]{:S(2)}, u32[]{:S(2)}) collective-permute-start(f32[1024,1152]{1,0:T(8,128)} %convolution_add_fusion.3), channel_id=1, source_target_pairs={{0,1},{1,2},{2,3},{3,4},{4,5},{5,6},{6,7},{7,8},{8,9},{9,10},{10,1... | collective-permute-start | bytes 14155784 | tf_op jit(solution)/shard_map/while/body/eval_jaxpr/ppermute | solution.py:48
  879.3 80.7 %collective-permute-start = (bf16[1024,1152]{1,0:T(8,128)(2,1)}, bf16[1024,1152]{1,0:T(8,128)(2,1)S(1)}, u32[]{:S(2)}, u32[]{:S(2)}) collective-permute-start(bf16[1024,1152]{1,0:T(8,128)(2,1)} %copy.23), channel_id=1, source_target_pairs={{0,1},{1,2},{2,3},{3,4},{4,5},{5,6},{6,7},{7,8},{8,9},{9,10},{10,1... | collective-permute-start | bytes 7077896 | tf_op jit(solution)/shard_map/while/body/eval_jaxpr/ppermute | solution.py:48
  982.4 80.7 %collective-permute-start.2 = (f32[1024,1152]{1,0:T(8,128)}, f32[1024,1152]{1,0:T(8,128)}, u32[]{:S(2)}, u32[]{:S(2)}) collective-permute-start(f32[1024,1152]{1,0:T(8,128)} %convolution_add_fusion.3), channel_id=1, source_target_pairs={{0,1},{1,2},{2,3},{3,4},{4,5},{5,6},{6,7},{7,8},{8,9},{9,10},{10,1... | collective-permute-start | bytes 14155784 | tf_op jit(solution)/shard_map/while/body/eval_jaxpr/ppermute | solution.py:48
  982.4 80.7 %collective-permute-start = (bf16[1024,1152]{1,0:T(8,128)(2,1)}, bf16[1024,1152]{1,0:T(8,128)(2,1)S(1)}, u32[]{:S(2)}, u32[]{:S(2)}) collective-permute-start(bf16[1024,1152]{1,0:T(8,128)(2,1)} %copy.23), channel_id=1, source_target_pairs={{0,1},{1,2},{2,3},{3,4},{4,5},{5,6},{6,7},{7,8},{8,9},{9,10},{10,1... | collective-permute-start | bytes 7077896 | tf_op jit(solution)/shard_map/while/body/eval_jaxpr/ppermute | solution.py:48
  1085.4 80.7 %collective-permute-start.2 = (f32[1024,1152]{1,0:T(8,128)}, f32[1024,1152]{1,0:T(8,128)}, u32[]{:S(2)}, u32[]{:S(2)}) collective-permute-start(f32[1024,1152]{1,0:T(8,128)} %convolution_add_fusion.3), channel_id=1, source_target_pairs={{0,1},{1,2},{2,3},{3,4},{4,5},{5,6},{6,7},{7,8},{8,9},{9,10},{10,1... | collective-permute-start | bytes 14155784 | tf_op jit(solution)/shard_map/while/body/eval_jaxpr/ppermute | solution.py:48
  1085.4 80.7 %collective-permute-start = (bf16[1024,1152]{1,0:T(8,128)(2,1)}, bf16[1024,1152]{1,0:T(8,128)(2,1)S(1)}, u32[]{:S(2)}, u32[]{:S(2)}) collective-permute-start(bf16[1024,1152]{1,0:T(8,128)(2,1)} %copy.23), channel_id=1, source_target_pairs={{0,1},{1,2},{2,3},{3,4},{4,5},{5,6},{6,7},{7,8},{8,9},{9,10},{10,1... | collective-permute-start | bytes 7077896 | tf_op jit(solution)/shard_map/while/body/eval_jaxpr/ppermute | solution.py:48
  1188.5 80.7 %collective-permute-start.2 = (f32[1024,1152]{1,0:T(8,128)}, f32[1024,1152]{1,0:T(8,128)}, u32[]{:S(2)}, u32[]{:S(2)}) collective-permute-start(f32[1024,1152]{1,0:T(8,128)} %convolution_add_fusion.3), channel_id=1, source_target_pairs={{0,1},{1,2},{2,3},{3,4},{4,5},{5,6},{6,7},{7,8},{8,9},{9,10},{10,1... | collective-permute-start | bytes 14155784 | tf_op jit(solution)/shard_map/while/body/eval_jaxpr/ppermute | solution.py:48
  1188.5 80.7 %collective-permute-start = (bf16[1024,1152]{1,0:T(8,128)(2,1)}, bf16[1024,1152]{1,0:T(8,128)(2,1)S(1)}, u32[]{:S(2)}, u32[]{:S(2)}) collective-permute-start(bf16[1024,1152]{1,0:T(8,128)(2,1)} %copy.23), channel_id=1, source_target_pairs={{0,1},{1,2},{2,3},{3,4},{4,5},{5,6},{6,7},{7,8},{8,9},{9,10},{10,1... | collective-permute-start | bytes 7077896 | tf_op jit(solution)/shard_map/while/body/eval_jaxpr/ppermute | solution.py:48
  1291.5 80.7 %collective-permute-start.2 = (f32[1024,1152]{1,0:T(8,128)}, f32[1024,1152]{1,0:T(8,128)}, u32[]{:S(2)}, u32[]{:S(2)}) collective-permute-start(f32[1024,1152]{1,0:T(8,128)} %convolution_add_fusion.3), channel_id=1, source_target_pairs={{0,1},{1,2},{2,3},{3,4},{4,5},{5,6},{6,7},{7,8},{8,9},{9,10},{10,1... | collective-permute-start | bytes 14155784 | tf_op jit(solution)/shard_map/while/body/eval_jaxpr/ppermute | solution.py:48
  1291.5 80.7 %collective-permute-start = (bf16[1024,1152]{1,0:T(8,128)(2,1)}, bf16[1024,1152]{1,0:T(8,128)(2,1)S(1)}, u32[]{:S(2)}, u32[]{:S(2)}) collective-permute-start(bf16[1024,1152]{1,0:T(8,128)(2,1)} %copy.23), channel_id=1, source_target_pairs={{0,1},{1,2},{2,3},{3,4},{4,5},{5,6},{6,7},{7,8},{8,9},{9,10},{10,1... | collective-permute-start | bytes 7077896 | tf_op jit(solution)/shard_map/while/body/eval_jaxpr/ppermute | solution.py:48
  1394.5 80.7 %collective-permute-start.2 = (f32[1024,1152]{1,0:T(8,128)}, f32[1024,1152]{1,0:T(8,128)}, u32[]{:S(2)}, u32[]{:S(2)}) collective-permute-start(f32[1024,1152]{1,0:T(8,128)} %convolution_add_fusion.3), channel_id=1, source_target_pairs={{0,1},{1,2},{2,3},{3,4},{4,5},{5,6},{6,7},{7,8},{8,9},{9,10},{10,1... | collective-permute-start | bytes 14155784 | tf_op jit(solution)/shard_map/while/body/eval_jaxpr/ppermute | solution.py:48
  1394.5 80.7 %collective-permute-start = (bf16[1024,1152]{1,0:T(8,128)(2,1)}, bf16[1024,1152]{1,0:T(8,128)(2,1)S(1)}, u32[]{:S(2)}, u32[]{:S(2)}) collective-permute-start(bf16[1024,1152]{1,0:T(8,128)(2,1)} %copy.23), channel_id=1, source_target_pairs={{0,1},{1,2},{2,3},{3,4},{4,5},{5,6},{6,7},{7,8},{8,9},{9,10},{10,1... | collective-permute-start | bytes 7077896 | tf_op jit(solution)/shard_map/while/body/eval_jaxpr/ppermute | solution.py:48
  1394.6 80.7 %collective-permute-start.1 = (s32[1024]{0:T(1024)S(1)}, s32[1024]{0:T(1024)S(1)}, u32[]{:S(2)}, u32[]{:S(2)}) collective-permute-start(s32[1024]{0:T(1024)S(1)} %copy.24), channel_id=1, source_target_pairs={{0,1},{1,2},{2,3},{3,4},{4,5},{5,6},{6,7},{7,8},{8,9},{9,10},{10,1... | collective-permute-start | bytes 12296 | tf_op jit(solution)/shard_map/while/body/eval_jaxpr/ppermute | solution.py:48
  1497.6 80.7 %collective-permute-start.2 = (f32[1024,1152]{1,0:T(8,128)}, f32[1024,1152]{1,0:T(8,128)}, u32[]{:S(2)}, u32[]{:S(2)}) collective-permute-start(f32[1024,1152]{1,0:T(8,128)} %convolution_add_fusion.3), channel_id=1, source_target_pairs={{0,1},{1,2},{2,3},{3,4},{4,5},{5,6},{6,7},{7,8},{8,9},{9,10},{10,1... | collective-permute-start | bytes 14155784 | tf_op jit(solution)/shard_map/while/body/eval_jaxpr/ppermute | solution.py:48
  1497.6 80.7 %collective-permute-start = (bf16[1024,1152]{1,0:T(8,128)(2,1)}, bf16[1024,1152]{1,0:T(8,128)(2,1)S(1)}, u32[]{:S(2)}, u32[]{:S(2)}) collective-permute-start(bf16[1024,1152]{1,0:T(8,128)(2,1)} %copy.23), channel_id=1, source_target_pairs={{0,1},{1,2},{2,3},{3,4},{4,5},{5,6},{6,7},{7,8},{8,9},{9,10},{10,1... | collective-permute-start | bytes 7077896 | tf_op jit(solution)/shard_map/while/body/eval_jaxpr/ppermute | solution.py:48
  (62 other events, 1658.9 us)
Sparse Core Ops, SparseCore 0:
  1659.0 130.7 all-reduce.3
where the time goes:
time: 1820 us; the launch traced here: 1810 us
  waiting for transfers between devices  1150 us (63%)
  matrix products  511 us (28%)
  local copies, waits for them, and re-layouts  57.8 us (3%)
  blocking collectives  33.4 us (2%)
  loops' own time  29.3 us (2%)
  between operations  21.5 us (1%)
    ppermute x45, waiting for transfers between devices, visit_block(): lax.ppermute((txt_blk, ids_blk, acc_txt + part_txt), 'data', next_perm)  1020 us
    dot_general x16, matrix products, tile_terms(): part_img = jnp.dot(grad_bf, emb_txt, preferred_element_type=jnp.float32)  170 us
    dot_general x16, matrix products, tile_terms(): lax.dot_general(emb_img, emb_txt, CONTRACT_COLS, preferred_element_type=j...  158 us
    dot_general x16, matrix products, tile_terms(): lax.dot_general(grad_bf, emb_img, CONTRACT_ROWS, preferred_element_type=j...  156 us
    psum x1, waiting for transfers between devices, local_fn(): lax.psum((loss_sum + loss_part, temp_sum + temp_part, bias_sum + bias_par...  94.3 us
    ppermute x1, waiting for transfers between devices, local_fn(): home_txt = lax.ppermute(acc_txt + part_txt, 'data', next_perm)  38.9 us
    while x90, local copies, waits for them, and re-layouts  37.7 us
  transfers between devices with their start and end apart: 47, of which 17 were waited for; matrix products, arithmetic and copies ran while one was open for 10% of the time, Pallas kernels for 0%

commit v1 on v0

v1 whole, which is shorter than its diff:
```python
import functools

import jax
import jax.numpy as jnp
from jax import lax
from jax.experimental import pallas as pl
from jax.experimental.pallas import tpu as pltpu
from jax.sharding import PartitionSpec as P

CONTRACT_ROWS = (((0,), (0,)), ((), ()))
CONTRACT_COLS = (((1,), (1,)), ((), ()))
LOG2E = 1.4426950408889634


def embed_rows(feat_rows, weights):
    raw_emb = jnp.dot(feat_rows, weights, preferred_element_type=jnp.float32)
    inv_norm = lax.rsqrt(jnp.sum(raw_emb * raw_emb, axis=1, keepdims=True))
    unit_emb = raw_emb * inv_norm
    return unit_emb, inv_norm, unit_emb.astype(jnp.bfloat16)


def weight_grad(feat_rows, unit_emb, inv_norm, grad_emb):
    raw_grad = inv_norm * (grad_emb - unit_emb * jnp.sum(unit_emb * grad_emb, axis=1, keepdims=True))
    return lax.dot_general(feat_rows, raw_grad.astype(jnp.bfloat16), CONTRACT_ROWS, preferred_element_type=jnp.float32)


def pair_kernel(want, first, sub, scal, own, rem, ids_own, ids_rem, *refs):
    n_in = 0 if first else (4 if want else 1)
    prev, outs = refs[:n_in], refs[n_in:]
    acc = outs[0]

    @pl.when(pl.program_id(0) == 0)
    def _():
        for i, out in enumerate(outs):
            out[...] = jnp.zeros_like(out) if first else prev[i][...]

    neg_scale, neg_bias = scal[0], scal[1]
    rem_rows = rem.shape[0]
    n_sub = rem_rows // sub

    def sim(k):
        return lax.dot_general(own[...], rem[k * sub:(k + 1) * sub, :], CONTRACT_COLS, preferred_element_type=jnp.float32)

    def fold(x):
        y = x[:, 0:128]
        for c in range(1, sub // 128):
            y = y + x[:, c * 128:(c + 1) * 128]
        return jnp.sum(y.reshape(-1, 8, 128), axis=0)

    sims = [sim(0)]
    grads = []
    for k in range(n_sub):
        if k + 1 < n_sub:
            sims.append(sim(k + 1))
        pos = ids_own[...] == ids_rem[:, k * sub:(k + 1) * sub]
        neg_y = jnp.where(pos, -1.0, 1.0)
        yz = (sims[k] * neg_scale + neg_bias) * neg_y
        if want:
            e = jnp.exp2(-jnp.abs(yz))
            r = 1.0 / (1.0 + e)
            grad = jnp.where(yz <= 0, r, e * r) * neg_y
            outs[1][...] += fold(jnp.log1p(e)) * LOG2E - fold(jnp.minimum(yz, 0.0))
            outs[2][...] += fold(grad * sims[k])
            outs[3][...] += fold(grad)
        else:
            grad = neg_y / (1.0 + jnp.exp2(yz))
        grads.append(grad.astype(jnp.bfloat16))
    acc[...] += jnp.dot(jnp.concatenate(grads, axis=1) if n_sub > 1 else grads[0], rem[...],
                        preferred_element_type=jnp.float32)


def pair_call(own, rem, ids_own, ids_rem, scal, prev, want, blk, sub):
    rows, dim = own.shape
    n_rem = rem.shape[0]
    first = prev is None
    outs = [jax.ShapeDtypeStruct((rows, dim), jnp.float32)]
    specs = [pl.BlockSpec((rows, dim), lambda j: (0, 0))]
    if want:
        outs += [jax.ShapeDtypeStruct((8, 128), jnp.float32)] * 3
        specs += [pl.BlockSpec((8, 128), lambda j: (0, 0))] * 3
    in_specs = [pl.BlockSpec(memory_space=pltpu.SMEM),
                pl.BlockSpec((rows, dim), lambda j: (0, 0)),
                pl.BlockSpec((blk, dim), lambda j: (j, 0)),
                pl.BlockSpec((rows, 1), lambda j: (0, 0)),
                pl.BlockSpec((1, blk), lambda j: (0, j))]
    args = [scal, own, rem, ids_own, ids_rem]
    alias = {}
    if not first:
        in_specs += specs
        args += list(prev)
        alias = {5 + i: i for i in range(len(outs))}
    return pl.pallas_call(
        functools.partial(pair_kernel, want, first, sub),
        grid=(n_rem // blk,), in_specs=in_specs, out_specs=specs, out_shape=outs,
        input_output_aliases=alias,
        compiler_params=pltpu.CompilerParams(vmem_limit_bytes=56 << 20),
        cost_estimate=pl.CostEstimate(flops=4 * rows * n_rem * dim, bytes_accessed=2 * n_rem * dim, transcendentals=0),
    )(*args)


def solution(mesh):
    n_dev = mesh.shape["data"]
    chunks = 2

    def local_fn(feat_img, feat_txt, w_img, w_txt, log_temp, logit_bias, pair_ids):
        rows = feat_img.shape[0]
        dim = w_img.shape[1]
        total_rows = rows * n_dev
        temp_scale = jnp.exp(log_temp)
        scal = jnp.stack([-temp_scale * LOG2E, -logit_bias * LOG2E])
        unit_txt, inv_txt, emb_txt = embed_rows(feat_txt, w_txt)
        unit_img, inv_img, emb_img = embed_rows(feat_img, w_img)
        part = rows // chunks
        ids_all = lax.all_gather(pair_ids, "data")
        ids_own = pair_ids[:, None]

        def run_pass(own, other, want, sub):
            state = None
            for c in range(chunks):
                gathered = lax.all_gather(other[c * part:(c + 1) * part], "data", tiled=True)
                ids_rem = ids_all[:, c * part:(c + 1) * part].reshape(1, -1)
                state = pair_call(own, gathered, ids_own, ids_rem, scal, state, want, 1024, sub)
            return state

        acc_img, loss_sum, temp_sum, bias_sum = run_pass(emb_img, emb_txt, True, 256)
        (acc_txt,) = run_pass(emb_txt, emb_img, False, 512)
        factor = temp_scale / total_rows
        dw_img = weight_grad(feat_img, unit_img, inv_img, factor * acc_img)
        dw_txt = weight_grad(feat_txt, unit_txt, inv_txt, factor * acc_txt)
        sums = jnp.stack([jnp.sum(loss_sum), jnp.sum(temp_sum), jnp.sum(bias_sum)])
        sums, dw_img, dw_txt = lax.psum((sums, dw_img, dw_txt), "data")
        return (sums[0] / (LOG2E * total_rows), temp_scale * sums[1] / total_rows, sums[2] / total_rows, dw_img, dw_txt)

    return jax.shard_map(
        local_fn,
        mesh=mesh,
        in_specs=(P("data", None), P("data", None), P(None, None), P(None, None), P(), P(), P("data")),
        out_specs=(P(), P(), P(), P(None, None), P(None, None)),
        check_vma=False,
    )
```

time: 1820 us -> 604 us (0.33)
  waiting for transfers between devices: 1150 us -> 218 us
  matrix products: 511 us -> 23.6 us
  Pallas kernels: 0 us -> 248 us
  local copies, waits for them, and re-layouts: 57.8 us -> 26.8 us
  loops' own time: 29.3 us -> 0 us
    ppermute x46 -> x0, waiting for transfers between devices: 1050 us -> none  [the longest x45 1020 us: visit_block(): lax.ppermute((txt_blk, ids_blk, acc_txt + part_txt), 'data', next_perm)]
    dot_general x48 -> x0, matrix products: 483 us -> none  [the longest x16 170 us: tile_terms(): part_img = jnp.dot(grad_bf, emb_txt, preferred_element_type=jnp.float32)]
    pallas_call x0 -> x4, Pallas kernels: none -> 248 us  [pair_call(): pl.pallas_call(functools.partial(pair_kernel, want, first, sub), grid=(n_...]
    all_gather x0 -> x4, waiting for transfers between devices: none -> 125 us  [run_pass(): lax.all_gather(other[c * part:(c + 1) * part], 'data', tiled=True)]
    while x90 -> x0, local copies, waits for them, and re-layouts: 37.7 us -> none
    another operation x1 -> x0, loops' own time: 29.3 us -> none  [local_fn(): loop_state = lax.fori_loop(0, n_dev - 1, visit_block, loop_state)]
  transfers between devices with their start and end apart: 47 -> 5, of which waited for: 17 -> 5; matrix products, arithmetic and copies ran while one was open for 10% -> 4% of each run, Pallas kernels for 0% -> 29%
where the time goes in v1:
time: 604 us; the launch traced here: 598 us
  Pallas kernels  248 us (41%)
  waiting for transfers between devices  218 us (36%)
  blocking collectives  47.6 us (8%)
  local copies, waits for them, and re-layouts  26.8 us (4%)
  matrix products  23.6 us (4%)
  between operations  21.1 us (3%)
  other arithmetic  12.9 us (2%)
    pallas_call x4, Pallas kernels, pair_call(): pl.pallas_call(functools.partial(pair_kernel, want, first, sub), grid=(n_...  248 us
    all_gather x4, waiting for transfers between devices, run_pass(): lax.all_gather(other[c * part:(c + 1) * part], 'data', tiled=True)  125 us
    psum x1, waiting for transfers between devices, local_fn(): sums, dw_img, dw_txt = lax.psum((sums, dw_img, dw_txt), 'data')  91.4 us
    psum x1, blocking collectives, local_fn(): sums, dw_img, dw_txt = lax.psum((sums, dw_img, dw_txt), 'data')  32.5 us
    unnamed x45, local copies, waits for them, and re-layouts  21.3 us
    all_gather x1, blocking collectives, local_fn(): ids_all = lax.all_gather(pair_ids, 'data')  15.1 us
    dot_general x2, matrix products, weight_grad(): lax.dot_general(feat_rows, raw_grad.astype(jnp.bfloat16), CONTRACT_ROWS,...  12.1 us
  transfers between devices with their start and end apart: 5, of which 5 were waited for; matrix products, arithmetic and copies ran while one was open for 4% of the time, Pallas kernels for 29%

profile of v1, /device:TPU:0, one launch (start us, length us, event | category | flops | bytes accessed | tf_op | source)
XLA Modules:
  0.0 597.8 jit_solution(3321422367466213253)
XLA Ops:
  7.2 1.7 copy-done
  8.9 5.3 multiply_reduce_fusion.3
  14.6 1.9 fusion.6
  16.5 0.7 copy-done.2
  17.3 0.7 all-gather.10.cloned.1.call-update
  18.0 6.1 %multiply_reduce_fusion.2 = (f32[1024]{0:T(1024)S(1)}, f32[1024,1152]{1,0:T(8,128)S(1)}) fusion(bf16[1024,1152]{1,0:T(8,128)(2,1)} %param.8, bf16[1152,1152]{1,0:T(8,128)(2,1)} %param.10), kind=kOutput, calls=%fused_computation.6 | convolution fusion | flops 2720267264 | bytes 9736192 | tf_op jit(solution)/shard_map/dot_general | solution.py:16
  24.5 2.0 fusion.7
  29.0 1.0 copy.26.ids_own
  30.1 15.1 %all-gather = s32[16384]{0:T(1024)S(1)} all-gather(s32[1024]{0:T(1024)S(1)} %copy-done.10), channel_id=2, replica_groups=mesh['data'=16] {'data'}, dimensions={0}, use_global_device_ids=true | all-gather | bytes 69632 | tf_op jit(solution)/shard_map/all_gather | solution.py:114
  45.2 0.6 copy.32
  45.8 0.6 copy.31
  47.0 56.2 %all-gather.12.cloned.1.call-done.rem = bf16[8192,1152]{1,0:T(8,128)(2,1)} async-done(((bf16[512,1152]{1,0:T(8,128)(2,1)}), bf16[8192,1152]{1,0:T(8,128)(2,1)}) %all-gather.12.cloned.1.call-update) | async-done | bytes 18874384 | tf_op jit(solution)/shard_map/all_gather | solution.py:120
  103.2 50.4 %shard_map.112.refs_0_ = f32[1024,1152]{1,0:T(8,128)} custom-call(f32[2]{0:T(128)} %pad_maximum_fusion.scal, bf16[1024,1152]{1,0:T(8,128)(2,1)} %copy-done.5, bf16[8192,1152]{1,0:T(8,128)(2,1)} %all-gather.12.cloned.1.call-done.rem, s32[1024,1]{1,0:T(8,128)} %copy.26.ids_own, s32[1,8192]{1,0:T(1,128)} %bitcast.33), custom_call_target="tpu_custom_call" | custom-call | flops 38654705664 | bytes 18874368 | tf_op jit(solution)/shard_map/pallas_call | solution.py:92
  153.7 34.7 %all-gather.10.cloned.1.call-done.rem = bf16[8192,1152]{1,0:T(8,128)(2,1)} async-done(((bf16[512,1152]{1,0:T(8,128)(2,1)}), bf16[8192,1152]{1,0:T(8,128)(2,1)}) %all-gather.10.cloned.1.call-update) | async-done | bytes 18874384 | tf_op jit(solution)/shard_map/all_gather | solution.py:120
  188.3 52.1 %shard_map.113 = f32[1024,1152]{1,0:T(8,128)} custom-call(f32[2]{0:T(128)} %pad_maximum_fusion.scal, bf16[1024,1152]{1,0:T(8,128)(2,1)} %copy-done.5, bf16[8192,1152]{1,0:T(8,128)(2,1)} %all-gather.10.cloned.1.call-done.rem, s32[1024,1]{1,0:T(8,128)} %copy.26.ids_own, s32[1,8192]{1,0:T(1,128)} %bitcast.31, ...), custom_call_target="tpu_custom_call", output_to_operand_aliasing={{}: (5, {})} | custom-call | flops 38654705664 | bytes 18874368 | tf_op jit(solution)/shard_map/pallas_call | solution.py:92
  240.4 4.6 multiply_reduce_fusion
  245.5 0.8 copy-done.14
  246.3 6.1 %convolution_bitcast_fusion = f32[1152,1152]{0,1:T(8,128)} fusion(bf16[1024,1152]{1,0:T(8,128)(2,1)S(1)} %copy-done.14, f32[1024,1152]{1,0:T(8,128)S(1)} %copy-done.7, f32[1024,1152]{1,0:T(8,128)S(1)} %bitcast.30, f32[1024]{0:T(1024)S(1)} %multiply_reduce_fusion, f32[]{:T(128)S(6)} %div.21, f32[1024]{0:T(1024)S(1)} %rsqrt.17), kind=kOutput, calls=%fused_computation | convolution fusion | flops 2724986880 | bytes 17113092 | tf_op jit(solution)/shard_map/dot_general | solution.py:24
  252.3 21.0 %all-gather.8.cloned.1.call-done.rem = bf16[8192,1152]{1,0:T(8,128)(2,1)} async-done(((bf16[512,1152]{1,0:T(8,128)(2,1)}), bf16[8192,1152]{1,0:T(8,128)(2,1)}) %all-gather.8.cloned.1.call-update) | async-done | bytes 18874384 | tf_op jit(solution)/shard_map/all_gather | solution.py:120
  273.4 71.8 %shard_map.110 = (f32[1024,1152]{1,0:T(8,128)}, f32[8,128]{1,0:T(8,128)}, f32[8,128]{1,0:T(8,128)}, f32[8,128]{1,0:T(8,128)}) custom-call(f32[2]{0:T(128)} %pad_maximum_fusion.scal, bf16[1024,1152]{1,0:T(8,128)(2,1)} %copy-done.4, bf16[8192,1152]{1,0:T(8,128)(2,1)} %all-gather.8.cloned.1.call-done.rem, s32[1024,1]{1,0:T(8,128)} %copy.26.ids_own, ...), custom_call_target="tpu_custom_call" | custom-call | flops 38654705664 | bytes 18874368 | tf_op jit(solution)/shard_map/pallas_call | solution.py:92
  345.2 13.2 %all-gather.6.cloned.1.call-done.rem = bf16[8192,1152]{1,0:T(8,128)(2,1)} async-done(((bf16[512,1152]{1,0:T(8,128)(2,1)}), bf16[8192,1152]{1,0:T(8,128)(2,1)}) %all-gather.6.cloned.1.call-update) | async-done | bytes 18874384 | tf_op jit(solution)/shard_map/all_gather | solution.py:120
  358.3 73.6 %shard_map.111 = (f32[1024,1152]{1,0:T(8,128)}, f32[8,128]{1,0:T(8,128)}, f32[8,128]{1,0:T(8,128)}, f32[8,128]{1,0:T(8,128)}) custom-call(f32[2]{0:T(128)} %pad_maximum_fusion.scal, bf16[1024,1152]{1,0:T(8,128)(2,1)} %copy-done.4, ...), custom_call_target="tpu_custom_call", output_to_operand_aliasing={{0}: (5, {}), {1}: (6, {}), {2}: (7, {}), {3}: (8, {})} | custom-call | flops 38654705664 | bytes 18874368 | tf_op jit(solution)/shard_map/pallas_call | solution.py:92
  432.0 3.2 multiply_reduce_fusion.1
  435.7 0.8 copy-done.15
  436.5 6.1 %convolution_bitcast_fusion.1 = f32[1152,1152]{0,1:T(8,128)} fusion(bf16[1024,1152]{1,0:T(8,128)(2,1)S(1)} %copy-done.15, f32[1024,1152]{1,0:T(8,128)S(1)} %copy-done.6, f32[1024,1152]{1,0:T(8,128)S(1)} %bitcast.28, f32[1024]{0:T(1024)S(1)} %multiply_reduce_fusion.1, f32[]{:T(128)S(6)} %div.21, f32[1024]{0:T(1024)S(1)} %copy-done.9), kind=kOutput, calls=%fused_computation.1 | convolution fusion | flops 2724986880 | bytes 17113092 | tf_op jit(solution)/shard_map/dot_general | solution.py:24
  442.6 0.7 copy-done.11
  443.8 0.6 reduce_sum.66
  445.0 2.0 pad_maximum_fusion.1
  447.0 32.5 %psum.21 = f32[3]{0:T(128)S(1)} all-reduce(f32[3]{0:T(128)S(1)} %pad_maximum_fusion.1), channel_id=1, replica_groups=mesh['data'=16] {'data'}, use_global_device_ids=true, to_apply=%region_5.0 | all-reduce | flops 3 | bytes 24 | tf_op jit(solution)/shard_map/psum | solution.py:131
  482.1 91.4 %all-reduce.3.cloned.1.call-done = (f32[1152,1152]{0,1:T(8,128)}, f32[1152,1152]{0,1:T(8,128)}) async-done(((f32[1152,1152]{0,1:T(8,128)}, f32[1152,1152]{0,1:T(8,128)}), (f32[1152,1152]{0,1:T(8,128)}, f32[1152,1152]{0,1:T(8,128)})) %all-reduce.3.cloned.1.call-update) | async-done | bytes 10616848 | tf_op jit(solution)/shard_map/psum | solution.py:131
  573.5 6.9 %copy.29 = f32[1152,1152]{1,0:T(8,128)} copy(f32[1152,1152]{0,1:T(8,128)} %get-tuple-element.36) | data formatting | bytes 10616832
  580.4 7.0 %copy.30 = f32[1152,1152]{1,0:T(8,128)} copy(f32[1152,1152]{0,1:T(8,128)} %get-tuple-element.37) | data formatting | bytes 10616832
  (56 shorter events, 5.4 us)
Async XLA Ops:
  7.2 1.8 copy-start
  7.2 96.1 %all-gather.12.cloned.1.call-start = ((), (), s32[]{:S(2)}) async-start(), calls=%async_computation.3 | async-start | bytes 20054016 | tf_op jit(solution)/shard_map/all_gather | solution.py:120
  14.2 3.0 copy-start.2
  14.2 2.9 copy-start.8
  14.6 9.5 %copy-start.4 = (bf16[1024,1152]{1,0:T(8,128)(2,1)}, bf16[1024,1152]{1,0:T(8,128)(2,1)S(1)}, u32[]{:S(2)}) copy-start(bf16[1024,1152]{1,0:T(8,128)(2,1)S(1)} %multiply_convert_fusion.3.own) | copy-start | bytes 7077892
  17.2 171.1 %all-gather.10.cloned.1.call-start = ((), (), s32[]{:S(2)}) async-start(), calls=%async_computation.2 | async-start | bytes 20054016 | tf_op jit(solution)/shard_map/all_gather | solution.py:120
  18.0 255.4 %all-gather.8.cloned.1.call-start = ((), (), s32[]{:S(2)}) async-start(), calls=%async_computation.1 | async-start | bytes 20054016 | tf_op jit(solution)/shard_map/all_gather | solution.py:120
  24.1 2.9 copy-start.3
  24.5 78.8 %copy-start.5 = (bf16[1024,1152]{1,0:T(8,128)(2,1)}, bf16[1024,1152]{1,0:T(8,128)(2,1)S(1)}, u32[]{:S(2)}) copy-start(bf16[1024,1152]{1,0:T(8,128)(2,1)S(1)} %multiply_convert_fusion.2.own) | copy-start | bytes 7077892
  24.5 4.5 copy-start.10
  27.0 331.3 %all-gather.6.cloned.1.call-start = ((), (), s32[]{:S(2)}) async-start(), calls=%async_computation | async-start | bytes 20054016 | tf_op jit(solution)/shard_map/all_gather | solution.py:120
  27.6 545.9 %all-reduce.3.cloned.1.call-start = ((), (), s32[]{:S(2)}) async-start(), calls=%async_computation.4 | async-start | bytes 21233664 | tf_op jit(solution)/shard_map/psum | solution.py:131
  103.2 141.8 %slice-start.2 = ((s8[4718592]{0:T(1024)(128)(4,1)}), s8[524288]{0:T(1024)(128)(4,1)S(1)}, s32[]{:S(2)}) async-start(s8[4718592]{0:T(1024)(128)(4,1)} %bitcast.29), calls=%async_computation.7 | async-start | bytes 1048576
  188.3 56.8 %slice-start.3 = ((s8[4718592]{0:T(1024)(128)(4,1)}), s8[4194304]{0:T(1024)(128)(4,1)S(1)}, s32[]{:S(2)}) async-start(s8[4718592]{0:T(1024)(128)(4,1)} %bitcast.29), calls=%async_computation.8 | async-start | bytes 8388608
  240.4 5.1 copy-start.7
  240.4 5.9 copy-start.14
  273.4 158.5 %slice-start = ((s8[4718592]{0:T(1024)(128)(4,1)}), s8[524288]{0:T(1024)(128)(4,1)S(1)}, s32[]{:S(2)}) async-start(s8[4718592]{0:T(1024)(128)(4,1)} %bitcast.27), calls=%async_computation.5 | async-start | bytes 1048576
  358.3 73.6 %slice-start.1 = ((s8[4718592]{0:T(1024)(128)(4,1)}), s8[4194304]{0:T(1024)(128)(4,1)S(1)}, s32[]{:S(2)}) async-start(s8[4718592]{0:T(1024)(128)(4,1)} %bitcast.27), calls=%async_computation.6 | async-start | bytes 8388608
  358.3 73.6 %copy-start.9 = (f32[1024]{0:T(1024)S(1)}, f32[1024]{0:T(1024)}, u32[]{:S(2)}) copy-start(f32[1024]{0:T(1024)} %copy-done.8) | copy-start | bytes 12292
  431.9 3.8 copy-start.6
  431.9 4.5 copy-start.15
  442.5 0.7 copy-start.11
  442.5 1.3 copy-start.12
  442.5 1.9 copy-start.13
  580.4 7.0 %copy-start.1 = (bf16[1152,1152]{1,0:T(8,128)(2,1)S(1)}, bf16[1152,1152]{1,0:T(8,128)(2,1)}, u32[]{:S(2)}) copy-start(bf16[1152,1152]{1,0:T(8,128)(2,1)} %param.9) | copy-start | bytes 7962628
Sparse Core Ops, SparseCore 0:
  17.3 85.8 all-gather.11
  105.5 82.8 all-gather.9
  190.5 82.8 all-gather.7
  275.5 82.8 all-gather.5
  442.7 130.7 all-reduce.2

commit v2 on v0

v2 whole, which is shorter than its diff:
```python
import functools

import jax
import jax.numpy as jnp
from jax import lax
from jax.experimental import pallas as pl
from jax.experimental.pallas import tpu as pltpu
from jax.sharding import PartitionSpec as P

CONTRACT_ROWS = (((0,), (0,)), ((), ()))
CONTRACT_COLS = (((1,), (1,)), ((), ()))
LOG2E = 1.4426950408889634
MESH_ID = pl.DeviceIdType.MESH

ROWS, DIM = 1024, 1152
TILE = 512
COLOR = DIM // 3
LINK_BITS = (2, 4, 8)
SLOTS = 16
ROW_PIECE = 32
D1_PIECE = (512, 256)
D2_PIECE = (512, 512)


def embed_rows(feat_rows, weights):
    raw_emb = jnp.dot(feat_rows, weights, preferred_element_type=jnp.float32)
    inv_norm = lax.rsqrt(jnp.sum(raw_emb * raw_emb, axis=1, keepdims=True))
    unit_emb = raw_emb * inv_norm
    return unit_emb, inv_norm, unit_emb.astype(jnp.bfloat16)


def weight_grad(feat_rows, unit_emb, inv_norm, grad_emb):
    raw_grad = inv_norm * (grad_emb - unit_emb * jnp.sum(unit_emb * grad_emb, axis=1, keepdims=True))
    return lax.dot_general(feat_rows, raw_grad.astype(jnp.bfloat16), CONTRACT_ROWS, preferred_element_type=jnp.float32)


def transfer_table(color):
    b0, b1, b2 = (LINK_BITS[(color + j) % 3] for j in range(3))
    return ((b0, 0), (b1, 0), (b1, b0), (b2, 0), (b2, b0), (b2, b1), (b2, b0 | b1))


def tile_order():
    order = [(0, 0), (1, 0), (0, 1), (1, 1)]
    groups = [((2, 4, 8), 0), ((2, 4, 8), 1), ((6, 10, 12), 0), ((6, 10, 12), 1), ((14,), 0), ((14,), 1)]
    for slots, half in groups:
        for slot in slots:
            order += [(slot, half), (slot | 1, half)]
    return order


ORDER = tile_order()
N_TILES = len(ORDER)


def interleave(first, second):
    i = j = 0
    while i < len(first) or j < len(second):
        if j >= len(second) or (i < len(first) and i * len(second) <= j * len(first)):
            first[i]()
            i += 1
        else:
            second[j]()
            j += 1


def d1_pieces(own, tile, sim_out):
    def piece(m, n):
        sim_out[m:m + D1_PIECE[0], n:n + D1_PIECE[1]] = lax.dot_general(
            own[m:m + D1_PIECE[0], :], tile[n:n + D1_PIECE[1], :], CONTRACT_COLS, preferred_element_type=jnp.float32)

    return [functools.partial(piece, m, n) for n in range(0, TILE, D1_PIECE[1]) for m in range(0, ROWS, D1_PIECE[0])]


def d2_pieces(grad, tile, acc):
    def piece(m, n, end):
        acc[m:m + D2_PIECE[0], n:end] += jnp.dot(
            grad[m:m + D2_PIECE[0], :], tile[:, n:end], preferred_element_type=jnp.float32)

    return [functools.partial(piece, m, n, min(n + D2_PIECE[1], DIM))
            for m in range(0, ROWS, D2_PIECE[0]) for n in range(0, DIM, D2_PIECE[1])]


def fold_cols(x):
    y = x[:, 0:128]
    for c in range(1, TILE // 128):
        y = y + x[:, c * 128:(c + 1) * 128]
    return y


def vpu_pieces(want, neg_scale, neg_bias, sim, grad_out, ids_own, ids_rem, sums):
    state = {}

    def add(name, value):
        state[name] = state[name] + value if name in state else value

    def piece(r0):
        s = sim[r0:r0 + ROW_PIECE, :]
        neg_y = jnp.where(ids_own[r0:r0 + ROW_PIECE, :] == ids_rem[...], -1.0, 1.0)
        yz = (s * neg_scale + neg_bias) * neg_y
        if want:
            e = jnp.exp2(-jnp.abs(yz))
            r = 1.0 / (1.0 + e)
            grad = jnp.where(yz <= 0, r, e * r) * neg_y
            low = jnp.minimum(yz, 0.0)
            gs = grad * s
            for i in range(0, ROW_PIECE, 8):
                e_i = e[i:i + 8]
                state["prod"] = state["prod"] + (e_i + state["prod"] * e_i) if "prod" in state else e_i
                add("low", low[i:i + 8])
                add("gs", gs[i:i + 8])
                add("g", grad[i:i + 8])
            if (r0 + ROW_PIECE) % 512 == 0:
                state["low"] = state["low"] - jnp.log1p(state.pop("prod")) * LOG2E
            if r0 + ROW_PIECE == ROWS:
                sums[0][...] -= fold_cols(state["low"])
                sums[1][...] += fold_cols(state["gs"])
                sums[2][...] += fold_cols(state["g"])
        else:
            grad = neg_y / (1.0 + jnp.exp2(yz))
        grad_out[r0:r0 + ROW_PIECE, :] = grad.astype(jnp.bfloat16)

    return [functools.partial(piece, r0) for r0 in range(0, ROWS, ROW_PIECE)]


def main_kernel(scal, emb_txt_hbm, emb_img_hbm, emb_txt, emb_img, ids_own, ids_row,
                acc_img, acc_txt, sum_l, sum_t, sum_b, gat,
                tiles, sim0, sim1, grad0, grad1, ids_all, ids_cur,
                send_sem, recv_sem, pair_send, pair_recv, ids_send, ids_recv, tile_sem):
    me = lax.axis_index("data")
    emb_hbm = (emb_txt_hbm, emb_img_hbm)
    sims, grads = (sim0, sim1), (grad0, grad1)
    sums = (sum_l, sum_t, sum_b)

    def flip(bit):
        return me + bit * (1 - 2 * lax.rem(lax.div(me, bit), 2))

    peer = {bit: flip(bit) for bit in (1, 2, 4, 8)}

    def xor_dev(slot):
        dev = me
        for bit in (1, 2, 4, 8):
            if slot & bit:
                dev = dev + (peer[bit] - me)
        return dev

    def rows_of(half):
        return pl.ds(half * TILE, TILE)

    def transfer(arr, half, color, i):
        link, slot = transfer_table(color)[i]
        cols = pl.ds(color * COLOR, COLOR)
        src = emb_hbm[arr].at[rows_of(half), cols] if slot == 0 else gat.at[arr, slot, rows_of(half), cols]
        return pltpu.make_async_remote_copy(
            src_ref=src, dst_ref=gat.at[arr, slot | link, rows_of(half), cols],
            send_sem=send_sem.at[arr, half, color, i], recv_sem=recv_sem.at[arr, half, color, i],
            device_id=(peer[link],), device_id_type=MESH_ID)

    def pair_copy(arr, half, slot):
        src = emb_hbm[arr].at[rows_of(half)] if slot == 0 else gat.at[arr, slot, rows_of(half)]
        return pltpu.make_async_remote_copy(
            src_ref=src, dst_ref=gat.at[arr, slot | 1, rows_of(half)],
            send_sem=pair_send.at[arr, half, slot // 2], recv_sem=pair_recv.at[arr, half, slot // 2],
            device_id=(peer[1],), device_id_type=MESH_ID)

    def ids_copy(slot):
        return pltpu.make_async_remote_copy(
            src_ref=ids_row, dst_ref=ids_all.at[slot], send_sem=ids_send.at[slot], recv_sem=ids_recv.at[slot],
            device_id=(xor_dev(slot),), device_id_type=MESH_ID)

    def send_own(arr, half):
        for j in range(3):
            for d in range(3):
                color = (d - j) % 3
                transfer(arr, half, color, (0, 1, 3)[j]).start()

    def arrived(arr, slot, half):
        if slot == 0:
            return
        if slot & 1:
            pair_copy(arr, half, slot - 1).wait_recv()
            return
        for color in range(3):
            table = transfer_table(color)
            for i, (link, src) in enumerate(table):
                if src | link == slot:
                    transfer(arr, half, color, i).wait_recv()
        for color in range(3):
            table = transfer_table(color)
            for i, (link, src) in enumerate(table):
                if src == slot:
                    transfer(arr, half, color, i).start()
        pair_copy(arr, half, slot).start()

    def tile_copy(u):
        arr, (slot, half) = u // N_TILES, ORDER[u % N_TILES]
        src = emb_hbm[arr].at[rows_of(half)] if slot == 0 else gat.at[arr, slot, rows_of(half)]
        return pltpu.make_async_copy(src, tiles.at[u % 4], tile_sem.at[u % 4])

    def comm(u):
        if u + 1 < 2 * N_TILES:
            arr, (slot, half) = (u + 1) // N_TILES, ORDER[(u + 1) % N_TILES]
            arrived(arr, slot, half)
            tile_copy(u + 1).start()
            if (arr, slot, half) == (0, 12, 1):
                for h in range(2):
                    send_own(1, h)
                    pair_copy(1, h, 0).start()
        if u < 2 * N_TILES:
            tile_copy(u).wait()
        if u >= 1:
            v = u - 1
            slot, half = ORDER[v % N_TILES]
            if v < N_TILES and half == 0 and slot:
                ids_copy(slot).wait_recv()
            src = ids_row if slot == 0 else ids_all.at[slot]
            ids_cur[...] = src[:, half * TILE:(half + 1) * TILE]

    neg_scale, neg_bias = scal[0], scal[1]

    def step(par, d1_arr, vpu_arr, d2_arr, cur_buf, old_buf):
        mxu, vpu = [], []
        if d1_arr is not None:
            mxu += d1_pieces((emb_img, emb_txt)[d1_arr], tiles.at[cur_buf], sims[par])
        if d2_arr is not None:
            mxu += d2_pieces(grads[par], tiles.at[old_buf], (acc_img, acc_txt)[d2_arr])
        if vpu_arr is not None:
            vpu = vpu_pieces(vpu_arr == 0, neg_scale, neg_bias, sims[1 - par], grads[1 - par], ids_own, ids_cur, sums)
        interleave(mxu, vpu)

    barrier = pltpu.get_barrier_semaphore()
    for slot in range(1, SLOTS):
        pl.semaphore_signal(barrier, inc=1, device_id=(xor_dev(slot),), device_id_type=MESH_ID)
    pl.semaphore_wait(barrier, SLOTS - 1)

    tile_copy(0).start()
    for slot in range(1, SLOTS):
        ids_copy(slot).start()
    for h in range(2):
        pair_copy(0, h, 0).start()
        send_own(0, h)

    acc_img[...] = jnp.zeros_like(acc_img)
    acc_txt[...] = jnp.zeros_like(acc_txt)
    for out in sums:
        out[...] = jnp.zeros_like(out)

    comm(0)
    step(0, 0, None, None, 0, 0)
    comm(1)
    step(1, 0, 0, None, 1, 0)

    def run_loop(arr, start):
        n_iter = (N_TILES - 2) // 2

        @pl.loop(0, n_iter)
        def _(it):
            flip_buf = lax.rem(it, 2)
            base = (start // 2) % 2
            buf = 2 * lax.rem(it + base, 2)
            for par in range(2):
                for k in range(n_iter):
                    pl.when(it == k)(functools.partial(comm, start + 2 * k + par))
                step(par, arr, arr, arr, buf + par, (2 - buf) + par)

    run_loop(0, 2)
    comm(N_TILES)
    step(0, 1, 0, 0, N_TILES % 4, (N_TILES - 2) % 4)
    comm(N_TILES + 1)
    step(1, 1, 1, 0, (N_TILES + 1) % 4, (N_TILES - 1) % 4)
    run_loop(1, N_TILES + 2)
    comm(2 * N_TILES)
    step(0, None, 1, 1, 0, (2 * N_TILES - 2) % 4)
    step(1, None, None, 1, 0, (2 * N_TILES - 1) % 4)

    for slot in range(1, SLOTS):
        ids_copy(slot).wait_send()
    for arr in range(2):
        for half in range(2):
            for color in range(3):
                for i in range(7):
                    transfer(arr, half, color, i).wait_send()
            for slot in range(0, SLOTS, 2):
                pair_copy(arr, half, slot).wait_send()


def main_call(scal, emb_txt, emb_img, ids):
    vmem = pl.BlockSpec(memory_space=pltpu.VMEM)
    hbm = pl.BlockSpec(memory_space=pl.ANY)
    f32 = jnp.float32
    return pl.pallas_call(
        main_kernel,
        in_specs=[pl.BlockSpec(memory_space=pltpu.SMEM), hbm, hbm, vmem, vmem, vmem, vmem],
        out_specs=[vmem] * 5 + [hbm],
        out_shape=[jax.ShapeDtypeStruct((ROWS, DIM), f32)] * 2 + [jax.ShapeDtypeStruct((8, 128), f32)] * 3
        + [jax.ShapeDtypeStruct((2, SLOTS, ROWS, DIM), jnp.bfloat16)],
        scratch_shapes=[
            pltpu.VMEM((4, TILE, DIM), jnp.bfloat16),
            pltpu.VMEM((ROWS, TILE), f32), pltpu.VMEM((ROWS, TILE), f32),
            pltpu.VMEM((ROWS, TILE), jnp.bfloat16), pltpu.VMEM((ROWS, TILE), jnp.bfloat16),
            pltpu.VMEM((SLOTS, 1, ROWS), jnp.int32), pltpu.VMEM((1, TILE), jnp.int32),
            pltpu.SemaphoreType.DMA((2, 2, 3, 7)), pltpu.SemaphoreType.DMA((2, 2, 3, 7)),
            pltpu.SemaphoreType.DMA((2, 2, 8)), pltpu.SemaphoreType.DMA((2, 2, 8)),
            pltpu.SemaphoreType.DMA((SLOTS,)), pltpu.SemaphoreType.DMA((SLOTS,)),
            pltpu.SemaphoreType.DMA((4,)),
        ],
        compiler_params=pltpu.CompilerParams(collective_id=0, has_side_effects=True, vmem_limit_bytes=60 << 20),
    )(scal, emb_txt, emb_img, emb_txt, emb_img, ids[:, None], ids[None, :])


def solution(mesh):
    n_dev = mesh.shape["data"]

    def local_fn(feat_img, feat_txt, w_img, w_txt, log_temp, logit_bias, pair_ids):
        total_rows = feat_img.shape[0] * n_dev
        temp_scale = jnp.exp(log_temp)
        scal = jnp.stack([-temp_scale * LOG2E, -logit_bias * LOG2E])
        unit_txt, inv_txt, emb_txt = embed_rows(feat_txt, w_txt)
        unit_img, inv_img, emb_img = embed_rows(feat_img, w_img)
        acc_img, acc_txt, loss_sum, temp_sum, bias_sum, _ = main_call(scal, emb_txt, emb_img, pair_ids)
        factor = temp_scale / total_rows
        dw_img = weight_grad(feat_img, unit_img, inv_img, factor * acc_img)
        dw_txt = weight_grad(feat_txt, unit_txt, inv_txt, factor * acc_txt)
        sums = jnp.stack([jnp.sum(loss_sum), jnp.sum(temp_sum), jnp.sum(bias_sum)])
        sums, dw_img, dw_txt = lax.psum((sums, dw_img, dw_txt), "data")
        return (sums[0] / (LOG2E * total_rows), temp_scale * sums[1] / total_rows, sums[2] / total_rows, dw_img, dw_txt)

    return jax.shard_map(
        local_fn,
        mesh=mesh,
        in_specs=(P("data", None), P("data", None), P(None, None), P(None, None), P(), P(), P("data")),
        out_specs=(P(), P(), P(), P(None, None), P(None, None)),
        check_vma=False,
    )
```

time: 1820 us -> 495 us (0.27)
  waiting for transfers between devices: 1150 us -> 90.4 us
  matrix products: 511 us -> 25.2 us
  Pallas kernels: 0 us -> 281 us
  local copies, waits for them, and re-layouts: 57.8 us -> 20.1 us
  loops' own time: 29.3 us -> 0 us
    ppermute x46 -> x0, waiting for transfers between devices: 1050 us -> none  [the longest x45 1020 us: visit_block(): lax.ppermute((txt_blk, ids_blk, acc_txt + part_txt), 'data', next_perm)]
    dot_general x48 -> x0, matrix products: 483 us -> none  [the longest x16 170 us: tile_terms(): part_img = jnp.dot(grad_bf, emb_txt, preferred_element_type=jnp.float32)]
    pallas_call x0 -> x1, Pallas kernels: none -> 281 us  [main_call(): pl.pallas_call(main_kernel, in_specs=[pl.BlockSpec(memory_space=pltpu.SME...]
    while x90 -> x0, local copies, waits for them, and re-layouts: 37.7 us -> none
    another operation x1 -> x0, loops' own time: 29.3 us -> none  [local_fn(): loop_state = lax.fori_loop(0, n_dev - 1, visit_block, loop_state)]
  transfers between devices with their start and end apart: 47 -> 1, of which waited for: 17 -> 1; matrix products, arithmetic and copies ran while one was open for 10% -> 1% of each run, Pallas kernels for 0% -> 0%
where the time goes in v2:
time: 495 us; the launch traced here: 488 us
  Pallas kernels  281 us (57%)
  waiting for transfers between devices  90.4 us (18%)
  blocking collectives  31.6 us (6%)
  matrix products  25.2 us (5%)
  between operations  21.3 us (4%)
  local copies, waits for them, and re-layouts  20.1 us (4%)
  other arithmetic  17.8 us (4%)
    pallas_call x1, Pallas kernels, main_call(): pl.pallas_call(main_kernel, in_specs=[pl.BlockSpec(memory_space=pltpu.SME...  281 us
    psum x1, waiting for transfers between devices, local_fn(): sums, dw_img, dw_txt = lax.psum((sums, dw_img, dw_txt), 'data')  90.4 us
    psum x1, blocking collectives, local_fn(): sums, dw_img, dw_txt = lax.psum((sums, dw_img, dw_txt), 'data')  31.6 us
    unnamed x36, local copies, waits for them, and re-layouts  18.4 us
    dot_general x2, matrix products, embed_rows(): raw_emb = jnp.dot(feat_rows, weights, preferred_element_type=jnp.float32)  12.7 us
    dot_general x2, matrix products, weight_grad(): lax.dot_general(feat_rows, raw_grad.astype(jnp.bfloat16), CONTRACT_ROWS,...  12.4 us
  transfers between devices with their start and end apart: 1, of which 1 were waited for; matrix products, arithmetic and copies ran while one was open for 1% of the time, Pallas kernels for 0%

profile of v2, /device:TPU:0, one launch (start us, length us, event | category | flops | bytes accessed | tf_op | source)
XLA Modules:
  0.0 487.5 jit_solution(1073685702746915582)
XLA Ops:
  7.2 0.0 copy-start
  7.2 0.0 all-reduce.3.cloned.1.call-start
  7.2 1.7 copy-done
  8.9 7.5 %multiply_reduce_fusion.2 = (f32[1024]{0:T(1024)S(1)}, f32[1024,1152]{1,0:T(8,128)}) fusion(bf16[1024,1152]{1,0:T(8,128)(2,1)} %param.7, bf16[1152,1152]{1,0:T(8,128)(2,1)S(1)} %copy-done), kind=kOutput, calls=%fused_computation.6 | convolution fusion | flops 2720267264 | bytes 9736192 | tf_op jit(solution)/shard_map/dot_general | solution.py:26
  16.4 0.0 copy-start.3
  16.5 5.2 %multiply_reduce_fusion.3 = (f32[1024]{0:T(1024)S(1)}, f32[1024,1152]{1,0:T(8,128)}) fusion(bf16[1024,1152]{1,0:T(8,128)(2,1)S(1)} %copy-done.8, bf16[1152,1152]{1,0:T(8,128)(2,1)S(1)} %copy-done.7), kind=kOutput, calls=%fused_computation.7 | convolution fusion | flops 2720267264 | bytes 9736192 | tf_op jit(solution)/shard_map/dot_general | solution.py:26
  23.0 1.1 copy.14.ids_own
  24.1 4.2 multiply_convert_fusion.2.emb_img_hbm.emb_img
  28.3 1.7 multiply_convert_fusion.3.emb_txt_hbm.emb_txt
  30.1 0.6 pad_maximum_fusion.scal
  30.7 281.2 %shard_map.110 = (f32[1024,1152]{1,0:T(8,128)}, f32[1024,1152]{1,0:T(8,128)}, f32[8,128]{1,0:T(8,128)}, f32[8,128]{1,0:T(8,128)}, f32[8,128]{1,0:T(8,128)}, /*index=5*/bf16[2,16,1024,1152]{3,2,1,0:T(8,128)(2,1)}) custom-call(f32[2]{0:T(128)} %pad_maximum_fusion.scal, bf16[1024,1152]{1,0:T(8,128)(2,1)} %multiply_convert_fusion.3.emb_txt_hbm.emb_txt, ...), custom_call_target="tpu_custom_call" | custom-call | tf_op jit(solution)/shard_map/pallas_call | solution.py:290
  311.9 0.0 slice-start.3
  311.9 0.0 copy-start.9
  311.9 0.0 slice-start
  311.9 0.0 slice-start.4
  311.9 7.4 %multiply_reduce_fusion = (f32[1024]{0:T(1024)S(1)}, f32[1024]{0:T(1024)S(1)}) fusion(f32[1024,1152]{1,0:T(8,128)} %get-tuple-element.14, f32[1024,1152]{1,0:T(8,128)} %get-tuple-element.31, f32[]{:T(128)S(6)} %div.21, f32[1024]{0:T(1024)S(1)} %rsqrt.16, f32[1024,1152]{1,0:T(8,128)} %get-tuple-element.13, f32[1024,1152]{1,0:T(8,128)} %get-tuple-element.33, ...), kind=kLoop, calls=%fused_computation.3 | loop fusion | flops 9435136 | bytes 18890756 | tf_op jit(solution)/shard_map/reduce_sum | solution.py:33
  319.4 0.1 slice-done.3
  319.5 1.4 copy-done.2
  320.9 0.7 copy-done.9
  321.6 6.2 %convolution_bitcast_fusion = f32[1152,1152]{0,1:T(8,128)} fusion(bf16[1024,1152]{1,0:T(8,128)(2,1)S(1)} %copy-done.9, f32[1024,1152]{1,0:T(8,128)S(1)} %copy-done.2, f32[1024,1152]{1,0:T(8,128)S(1)} %bitcast.23, f32[1024]{0:T(1024)S(1)} %get-tuple-element.34, f32[]{:T(128)S(6)} %div.21, f32[1024]{0:T(1024)S(1)} %rsqrt.16), kind=kOutput, calls=%fused_computation | convolution fusion | flops 2724986880 | bytes 17113092 | tf_op jit(solution)/shard_map/dot_general | solution.py:34
  327.9 6.2 %convolution_bitcast_fusion.1 = f32[1152,1152]{0,1:T(8,128)} fusion(bf16[1024,1152]{1,0:T(8,128)(2,1)S(1)} %copy-done.10, f32[1024,1152]{1,0:T(8,128)S(1)} %bitcast.25, f32[1024,1152]{1,0:T(8,128)S(1)} %bitcast.21, f32[1024]{0:T(1024)S(1)} %get-tuple-element.35, f32[]{:T(128)S(6)} %div.21, f32[1024]{0:T(1024)S(1)} %rsqrt.17), kind=kOutput, calls=%fused_computation.1 | convolution fusion | flops 2724986880 | bytes 17113092 | tf_op jit(solution)/shard_map/dot_general | solution.py:34
  334.1 0.0 all-reduce.3.cloned.1.call-update
  334.1 0.6 copy-done.6
  334.8 0.6 reduce_sum.65
  335.4 0.6 reduce_sum.66
  336.0 0.6 reduce_sum.67
  336.6 2.0 pad_maximum_fusion.1
  338.6 31.6 %psum.21 = f32[3]{0:T(128)S(1)} all-reduce(f32[3]{0:T(128)S(1)} %pad_maximum_fusion.1), channel_id=1, replica_groups=mesh['data'=16] {'data'}, use_global_device_ids=true, to_apply=%region_5.0 | all-reduce | flops 3 | bytes 24 | tf_op jit(solution)/shard_map/psum | solution.py:324
  370.2 0.6 fusion.6
  372.7 90.4 %all-reduce.3.cloned.1.call-done = (f32[1152,1152]{0,1:T(8,128)}, f32[1152,1152]{0,1:T(8,128)}) async-done(((f32[1152,1152]{0,1:T(8,128)}, f32[1152,1152]{0,1:T(8,128)}), (f32[1152,1152]{0,1:T(8,128)}, f32[1152,1152]{0,1:T(8,128)})) %all-reduce.3.cloned.1.call-update) | async-done | bytes 10616848 | tf_op jit(solution)/shard_map/psum | solution.py:324
  463.1 6.9 %copy.15 = f32[1152,1152]{1,0:T(8,128)} copy(f32[1152,1152]{0,1:T(8,128)} %get-tuple-element.25) | data formatting | bytes 10616832
  470.0 6.9 %copy.16 = f32[1152,1152]{1,0:T(8,128)} copy(f32[1152,1152]{0,1:T(8,128)} %get-tuple-element.26) | data formatting | bytes 10616832
  (28 shorter events, 0.1 us)
Async XLA Ops:
  7.2 1.8 copy-start
  7.2 455.9 %all-reduce.3.cloned.1.call-start = ((), (), s32[]{:S(2)}) async-start(), calls=%async_computation | async-start | bytes 21233664 | tf_op jit(solution)/shard_map/psum | solution.py:324
  8.9 7.5 %copy-start.7 = (bf16[1152,1152]{1,0:T(8,128)(2,1)S(1)}, bf16[1152,1152]{1,0:T(8,128)(2,1)}, u32[]{:S(2)}) copy-start(bf16[1152,1152]{1,0:T(8,128)(2,1)} %param.10) | copy-start | bytes 7962628
  8.9 7.5 %copy-start.8 = (bf16[1024,1152]{1,0:T(8,128)(2,1)S(1)}, bf16[1024,1152]{1,0:T(8,128)(2,1)}, u32[]{:S(2)}) copy-start(bf16[1024,1152]{1,0:T(8,128)(2,1)} %param.8) | copy-start | bytes 7077892
  16.4 6.6 %copy-start.3 = (s32[1024]{0:T(1024)S(1)}, s32[1024]{0:T(1024)}, u32[]{:S(2)}) copy-start(s32[1024]{0:T(1024)} %param.13) | copy-start | bytes 12292
  24.1 4.2 copy-start.1
  30.7 288.7 %slice-start.2 = ((s8[4718592]{0:T(1024)(128)(4,1)}), s8[524288]{0:T(1024)(128)(4,1)S(1)}, s32[]{:S(2)}) async-start(s8[4718592]{0:T(1024)(128)(4,1)} %bitcast.22), calls=%async_computation.3 | async-start | bytes 1048576
  311.9 7.6 %slice-start.3 = ((s8[4718592]{0:T(1024)(128)(4,1)}), s8[4194304]{0:T(1024)(128)(4,1)S(1)}, s32[]{:S(2)}) async-start(s8[4718592]{0:T(1024)(128)(4,1)} %bitcast.22), calls=%async_computation.4 | async-start | bytes 8388608
  311.9 9.1 %copy-start.2 = (f32[1024,1152]{1,0:T(8,128)S(1)}, f32[1024,1152]{1,0:T(8,128)}, u32[]{:S(2)}) copy-start(f32[1024,1152]{1,0:T(8,128)} %get-tuple-element.14) | copy-start | bytes 14155780
  311.9 9.7 %copy-start.9 = (bf16[1024,1152]{1,0:T(8,128)(2,1)S(1)}, bf16[1024,1152]{1,0:T(8,128)(2,1)}, u32[]{:S(2)}) copy-start(bf16[1024,1152]{1,0:T(8,128)(2,1)} %param.8) | copy-start | bytes 7077892
  311.9 15.9 %slice-start = ((s8[4718592]{0:T(1024)(128)(4,1)}), s8[524288]{0:T(1024)(128)(4,1)S(1)}, s32[]{:S(2)}) async-start(s8[4718592]{0:T(1024)(128)(4,1)} %bitcast.20), calls=%async_computation.1 | async-start | bytes 1048576
  311.9 15.9 %slice-start.4 = ((s8[4718592]{0:T(1024)(128)(4,1)}), s8[4194304]{0:T(1024)(128)(4,1)S(1)}, s32[]{:S(2)}) async-start(s8[4718592]{0:T(1024)(128)(4,1)} %bitcast.24), calls=%async_computation.5 | async-start | bytes 8388608
  321.6 6.2 %slice-start.1 = ((s8[4718592]{0:T(1024)(128)(4,1)}), s8[4194304]{0:T(1024)(128)(4,1)S(1)}, s32[]{:S(2)}) async-start(s8[4718592]{0:T(1024)(128)(4,1)} %bitcast.20), calls=%async_computation.2 | async-start | bytes 8388608
  321.6 6.2 %slice-start.5 = ((s8[4718592]{0:T(1024)(128)(4,1)}), s8[524288]{0:T(1024)(128)(4,1)S(1)}, s32[]{:S(2)}) async-start(s8[4718592]{0:T(1024)(128)(4,1)} %bitcast.24), calls=%async_computation.6 | async-start | bytes 1048576
  321.6 6.2 %copy-start.10 = (bf16[1024,1152]{1,0:T(8,128)(2,1)S(1)}, bf16[1024,1152]{1,0:T(8,128)(2,1)}, u32[]{:S(2)}) copy-start(bf16[1024,1152]{1,0:T(8,128)(2,1)} %param.7) | copy-start | bytes 7077892
  334.1 0.7 copy-start.6
  334.1 1.3 copy-start.5
  334.1 1.9 copy-start.4
Sparse Core Ops, SparseCore 0:
  334.3 128.8 all-reduce.2

commit v3 on v2

v3 whole, which is shorter than its diff:
```python
import functools

import jax
import jax.numpy as jnp
from jax import lax
from jax.experimental import pallas as pl
from jax.experimental.pallas import tpu as pltpu
from jax.sharding import PartitionSpec as P

CONTRACT_ROWS = (((0,), (0,)), ((), ()))
CONTRACT_COLS = (((1,), (1,)), ((), ()))
LOG2E = 1.4426950408889634
MESH_ID = pl.DeviceIdType.MESH

ROWS, DIM = 1024, 1152
TILE = 512
COLOR = DIM // 3
LINK_BITS = (2, 4, 8)
SLOTS = 16
ROW_PIECE = 32
D1_PIECE = (512, 256)
D2_PIECE = (512, 512)
HALF_DIM = DIM // 2
RS_ROWS = (HALF_DIM // 2, HALF_DIM // 4, HALF_DIM // 8)
REDUCE_STEPS = {50: 1, 53: 2, 55: 3, 57: 4, 59: 5, 61: 6, 64: 7}


def transfer_table(color):
    b0, b1, b2 = (LINK_BITS[(color + j) % 3] for j in range(3))
    return ((b0, 0), (b1, 0), (b1, b0), (b2, 0), (b2, b0), (b2, b1), (b2, b0 | b1))


def tile_order():
    order = [(0, 0), (1, 0), (0, 1), (1, 1)]
    groups = [((2, 4, 8), 0), ((2, 4, 8), 1), ((6, 10, 12), 0), ((6, 10, 12), 1), ((14,), 0), ((14,), 1)]
    for slots, half in groups:
        for slot in slots:
            order += [(slot, half), (slot | 1, half)]
    return order


ORDER = tile_order()
N_TILES = len(ORDER)


def interleave(first, second):
    i = j = 0
    while i < len(first) or j < len(second):
        if j >= len(second) or (i < len(first) and i * len(second) <= j * len(first)):
            first[i]()
            i += 1
        else:
            second[j]()
            j += 1


def d1_pieces(own, tile, sim_out):
    def piece(m, n):
        sim_out[m:m + D1_PIECE[0], n:n + D1_PIECE[1]] = lax.dot_general(
            own[m:m + D1_PIECE[0], :], tile[n:n + D1_PIECE[1], :], CONTRACT_COLS, preferred_element_type=jnp.float32)

    return [functools.partial(piece, m, n) for n in range(0, TILE, D1_PIECE[1]) for m in range(0, ROWS, D1_PIECE[0])]


def d2_pieces(grad, tile, acc):
    def piece(m, n, end):
        acc[m:m + D2_PIECE[0], n:end] += jnp.dot(
            grad[m:m + D2_PIECE[0], :], tile[:, n:end], preferred_element_type=jnp.float32)

    return [functools.partial(piece, m, n, min(n + D2_PIECE[1], DIM))
            for m in range(0, ROWS, D2_PIECE[0]) for n in range(0, DIM, D2_PIECE[1])]


def fold_cols(x):
    y = x[:, 0:128]
    for c in range(1, TILE // 128):
        y = y + x[:, c * 128:(c + 1) * 128]
    return y


def vpu_pieces(want, neg_scale, neg_bias, sim, grad_out, ids_own, ids_rem, sums):
    state = {}

    def add(name, value):
        state[name] = state[name] + value if name in state else value

    def piece(r0):
        s = sim[r0:r0 + ROW_PIECE, :]
        neg_y = jnp.where(ids_own[r0:r0 + ROW_PIECE, :] == ids_rem[...], -1.0, 1.0)
        yz = (s * neg_scale + neg_bias) * neg_y
        if want:
            e = jnp.exp2(-jnp.abs(yz))
            r = 1.0 / (1.0 + e)
            grad = jnp.where(yz <= 0, r, e * r) * neg_y
            low = jnp.minimum(yz, 0.0)
            gs = grad * s
            for i in range(0, ROW_PIECE, 8):
                e_i = e[i:i + 8]
                state["prod"] = state["prod"] + (e_i + state["prod"] * e_i) if "prod" in state else e_i
                add("low", low[i:i + 8])
                add("gs", gs[i:i + 8])
                add("g", grad[i:i + 8])
            if (r0 + ROW_PIECE) % 512 == 0:
                state["low"] = state["low"] - jnp.log1p(state.pop("prod")) * LOG2E
            if r0 + ROW_PIECE == ROWS:
                sums[0][...] -= fold_cols(state["low"])
                sums[1][...] += fold_cols(state["gs"])
                sums[2][...] += fold_cols(state["g"])
        else:
            grad = neg_y / (1.0 + jnp.exp2(yz))
        grad_out[r0:r0 + ROW_PIECE, :] = grad.astype(jnp.bfloat16)

    return [functools.partial(piece, r0) for r0 in range(0, ROWS, ROW_PIECE)]


def main_kernel(scal, feat_txt, feat_img, w_txt, w_img, ids_own, ids_row,
                dw_img, dw_txt, totals, gat, unit_hbm,
                feat0, feat1, wgt, part, unit, inv0, inv1, emb_txt, emb_img, acc_img, acc_txt,
                tiles, sim0, sim1, grad0, grad1, ids_all, ids_cur, sums_all, rx_pair, rx1, rx2, rx3,
                send_sem, recv_sem, pair_send, pair_recv, ids_send, ids_recv, tile_sem, load_sem, unit_sem, own_sem,
                sum_send, sum_recv, half_send, half_recv, ring_send, ring_recv):
    me = lax.axis_index("data")
    embs = (emb_txt, emb_img)
    feats, invs = (feat0, feat1), (inv0, inv1)
    sims, grads = (sim0, sim1), (grad0, grad1)
    sums = tuple(sums_all.at[0, i] for i in range(3))
    neg_scale, neg_bias, factor = scal[0], scal[1], scal[2]

    def bit_of(bit):
        return lax.rem(lax.div(me, bit), 2)

    peer = {bit: me + bit * (1 - 2 * bit_of(bit)) for bit in (1, 2, 4, 8)}

    def xor_dev(slot):
        dev = me
        for bit in (1, 2, 4, 8):
            if slot & bit:
                dev = dev + (peer[bit] - me)
        return dev

    def remote(src, dst, send, recv, dev):
        return pltpu.make_async_remote_copy(src_ref=src, dst_ref=dst, send_sem=send, recv_sem=recv,
                                            device_id=(dev,), device_id_type=MESH_ID)

    def rows_of(half):
        return pl.ds(half * TILE, TILE)

    def transfer(arr, half, color, i):
        link, slot = transfer_table(color)[i]
        cols = pl.ds(color * COLOR, COLOR)
        return remote(gat.at[arr, slot, rows_of(half), cols], gat.at[arr, slot | link, rows_of(half), cols],
                      send_sem.at[arr, half, color, i], recv_sem.at[arr, half, color, i], peer[link])

    def pair_copy(arr, half, slot):
        return remote(gat.at[arr, slot, rows_of(half)], gat.at[arr, slot | 1, rows_of(half)],
                      pair_send.at[arr, half, slot // 2], pair_recv.at[arr, half, slot // 2], peer[1])

    def ids_copy(slot):
        return remote(ids_row, ids_all.at[slot], ids_send.at[slot], ids_recv.at[slot], xor_dev(slot))

    def sums_copy(slot):
        return remote(sums_all.at[0], sums_all.at[slot], sum_send.at[slot], sum_recv.at[slot], xor_dev(slot))

    def send_own(arr, half):
        pair_copy(arr, half, 0).start()
        for j in range(3):
            for d in range(3):
                color = (d - j) % 3
                transfer(arr, half, color, (0, 1, 3)[j]).start()

    def arrived(arr, slot, half):
        if slot == 0:
            return
        if slot & 1:
            pair_copy(arr, half, slot - 1).wait_recv()
            return
        for color in range(3):
            for i, (link, src) in enumerate(transfer_table(color)):
                if src | link == slot:
                    transfer(arr, half, color, i).wait_recv()
        for color in range(3):
            for i, (link, src) in enumerate(transfer_table(color)):
                if src == slot:
                    transfer(arr, half, color, i).start()
        pair_copy(arr, half, slot).start()

    dws = (dw_img, dw_txt)
    rxs = (rx1, rx2, rx3)

    def half_copy(arr, last):
        core = bit_of(1)
        start = HALF_DIM * (core if last else 1 - core)
        src = (dws[arr] if last else part).at[pl.ds(pl.multiple_of(start, 8), HALF_DIM)]
        return remote(src, src if last else rx_pair, half_send.at[arr, last], half_recv.at[arr, last], peer[1])

    def ring_offset(color, depth, flip_last):
        off = HALF_DIM * bit_of(1)
        for j in range(depth):
            bit = bit_of(LINK_BITS[(color + j) % 3])
            if flip_last and j == depth - 1:
                bit = 1 - bit
            off = off + RS_ROWS[j] * bit
        return pl.multiple_of(off, 8)

    def ring_copy(arr, color, phase):
        cols = pl.ds(color * COLOR, COLOR)
        if phase < 3:
            rows = pl.ds(ring_offset(color, phase + 1, True), RS_ROWS[phase])
            src, dst, dim = part.at[rows, cols], rxs[phase].at[color], phase
        else:
            dim = 5 - phase
            rows = pl.ds(ring_offset(color, dim + 1, False), RS_ROWS[dim])
            src = dst = dws[arr].at[rows, cols]
        return remote(src, dst, ring_send.at[arr, color, phase], ring_recv.at[arr, color, phase],
                      peer[LINK_BITS[(color + dim) % 3]])

    def reduce_phase(arr, phase):
        if phase == 0:
            half_copy(arr, 0).start()
            return
        if phase == 1:
            half_copy(arr, 0).wait_recv()
            base = HALF_DIM * bit_of(1)

            @pl.loop(0, HALF_DIM // 32)
            def _(i):
                rows = pl.ds(pl.multiple_of(base + i * 32, 8), 32)
                part[rows, :] += rx_pair[pl.ds(pl.multiple_of(i * 32, 8), 32), :]

            for color in range(3):
                ring_copy(arr, color, 0).start()
            return
        if phase <= 4:
            done = phase - 2
            n_rows = RS_ROWS[done]
            for color in range(3):
                ring_copy(arr, color, done).wait_recv()
                cols = pl.ds(color * COLOR, COLOR)
                base = ring_offset(color, done + 1, False)

                @pl.loop(0, n_rows // 24)
                def _(i):
                    rows = pl.ds(pl.multiple_of(base + i * 24, 8), 24)
                    total = part[rows, cols] + rxs[done][color, pl.ds(pl.multiple_of(i * 24, 8), 24), :]
                    (dws[arr] if done == 2 else part)[rows, cols] = total

                ring_copy(arr, color, done + 1).start()
            return
        if phase <= 6:
            for color in range(3):
                ring_copy(arr, color, phase - 2).wait_recv()
                ring_copy(arr, color, phase - 1).start()
            return
        if phase == 7:
            for color in range(3):
                ring_copy(arr, color, 5).wait_recv()
            half_copy(arr, 1).start()
            return
        half_copy(arr, 1).wait_recv()
        for last in range(2):
            half_copy(arr, last).wait_send()
        for color in range(3):
            for ph in range(6):
                ring_copy(arr, color, ph).wait_send()

    def load(arr, which):
        src, dst = (((feat_txt, feat0), (w_txt, wgt)), ((feat_img, feat1), (w_img, wgt)))[arr][which]
        return pltpu.make_async_copy(src, dst, load_sem.at[arr, which])

    def own_copy(arr, half):
        return pltpu.make_async_copy(embs[arr].at[rows_of(half)], gat.at[arr, 0, rows_of(half)], own_sem.at[arr, half])

    def embed_half(arr, half):
        rows = rows_of(half)
        raw = jnp.dot(feats[arr][rows, :], wgt[...], preferred_element_type=jnp.float32)
        inv = lax.rsqrt(jnp.sum(raw * raw, axis=1, keepdims=True))
        unit_rows = raw * inv
        unit[rows, :] = unit_rows
        invs[arr][rows, :] = inv
        embs[arr][rows, :] = unit_rows.astype(jnp.bfloat16)
        own_copy(arr, half).start()

    def finish(arr, acc):
        @pl.loop(0, ROWS // 64)
        def _(i):
            rows = pl.ds(pl.multiple_of(i * 64, 64), 64)
            grad = factor * acc[rows, :]
            unit_rows = unit[rows, :]
            proj = jnp.sum(unit_rows * grad, axis=1, keepdims=True)
            embs[arr][rows, :] = (invs[arr][rows, :] * (grad - unit_rows * proj)).astype(jnp.bfloat16)

        part[...] = lax.dot_general(feats[arr][...], embs[arr][...], CONTRACT_ROWS, preferred_element_type=jnp.float32)

    def tile_copy(u):
        arr, (slot, half) = u // N_TILES, ORDER[u % N_TILES]
        return pltpu.make_async_copy(gat.at[arr, slot, rows_of(half)], tiles.at[u % 4], tile_sem.at[u % 4])

    def comm(u):
        if u + 1 < 2 * N_TILES:
            arr, (slot, half) = (u + 1) // N_TILES, ORDER[(u + 1) % N_TILES]
            arrived(arr, slot, half)
            tile_copy(u + 1).start()
            if (arr, slot, half) == (0, 12, 1):
                for h in range(2):
                    send_own(1, h)
        if u in REDUCE_STEPS:
            reduce_phase(0, REDUCE_STEPS[u])
        if u < 2 * N_TILES:
            tile_copy(u).wait()
        if u >= 1:
            v = u - 1
            slot, half = ORDER[v % N_TILES]
            if v < N_TILES and half == 0 and slot:
                ids_copy(slot).wait_recv()
            src = ids_row if slot == 0 else ids_all.at[slot]
            ids_cur[...] = src[:, half * TILE:(half + 1) * TILE]

    def step(par, d1_arr, vpu_arr, d2_arr, cur_buf, old_buf):
        mxu, vpu = [], []
        if d1_arr is not None:
            mxu += d1_pieces((emb_img, emb_txt)[d1_arr], tiles.at[cur_buf], sims[par])
        if d2_arr is not None:
            mxu += d2_pieces(grads[par], tiles.at[old_buf], (acc_img, acc_txt)[d2_arr])
        if vpu_arr is not None:
            vpu = vpu_pieces(vpu_arr == 0, neg_scale, neg_bias, sims[1 - par], grads[1 - par],
                             ids_own, ids_cur, sums)
        interleave(mxu, vpu)

    load(0, 0).start()
    load(0, 1).start()
    load(1, 0).start()
    barrier = pltpu.get_barrier_semaphore()
    for slot in range(1, SLOTS):
        pl.semaphore_signal(barrier, inc=1, device_id=(xor_dev(slot),), device_id_type=MESH_ID)
    load(0, 0).wait()
    load(0, 1).wait()
    embed_half(0, 0)
    pl.semaphore_wait(barrier, SLOTS - 1)
    own_copy(0, 0).wait()
    send_own(0, 0)
    tile_copy(0).start()
    for slot in range(1, SLOTS):
        ids_copy(slot).start()
    embed_half(0, 1)
    load(1, 1).start()
    own_copy(0, 1).wait()
    send_own(0, 1)
    unit_out = pltpu.make_async_copy(unit, unit_hbm, unit_sem.at[0])
    unit_out.start()
    acc_img[...] = jnp.zeros_like(acc_img)
    acc_txt[...] = jnp.zeros_like(acc_txt)
    for out in sums:
        out[...] = jnp.zeros(out.shape, jnp.float32)
    load(1, 0).wait()
    load(1, 1).wait()
    unit_out.wait()
    for half in range(2):
        embed_half(1, half)
    for half in range(2):
        own_copy(1, half).wait()

    comm(0)
    step(0, 0, None, None, 0, 0)
    comm(1)
    step(1, 0, 0, None, 1, 0)

    def run_loop(arr, start):
        n_iter = (N_TILES - 2) // 2

        @pl.loop(0, n_iter)
        def _(it):
            base = (start // 2) % 2
            buf = 2 * lax.rem(it + base, 2)
            for par in range(2):
                for k in range(n_iter):
                    pl.when(it == k)(functools.partial(comm, start + 2 * k + par))
                step(par, arr, arr, arr, buf + par, (2 - buf) + par)

    run_loop(0, 2)
    comm(N_TILES)
    step(0, 1, 0, 0, N_TILES % 4, (N_TILES - 2) % 4)
    for slot in range(1, SLOTS):
        sums_copy(slot).start()
    comm(N_TILES + 1)
    step(1, 1, 1, 0, (N_TILES + 1) % 4, (N_TILES - 1) % 4)
    finish(1, acc_img)
    reduce_phase(0, 0)
    unit_in = pltpu.make_async_copy(unit_hbm, unit, unit_sem.at[1])
    unit_in.start()
    run_loop(1, N_TILES + 2)
    comm(2 * N_TILES)
    step(0, None, 1, 1, 0, (2 * N_TILES - 2) % 4)
    step(1, None, None, 1, 0, (2 * N_TILES - 1) % 4)
    reduce_phase(0, 8)
    unit_in.wait()
    finish(0, acc_txt)
    reduce_phase(1, 0)

    for slot in range(1, SLOTS):
        sums_copy(slot).wait_recv()
    for i in range(3):
        parts = [sums_all[slot, i] for slot in range(SLOTS)]
        while len(parts) > 1:
            parts = [parts[j] + parts[j + 1] for j in range(0, len(parts), 2)]
        totals[i] = parts[0]
    for phase in range(1, 9):
        reduce_phase(1, phase)

    for slot in range(1, SLOTS):
        ids_copy(slot).wait_send()
        sums_copy(slot).wait_send()
    for arr in range(2):
        for half in range(2):
            for color in range(3):
                for i in range(7):
                    transfer(arr, half, color, i).wait_send()
            for slot in range(0, SLOTS, 2):
                pair_copy(arr, half, slot).wait_send()


def main_call(scal, feat_txt, feat_img, w_txt, w_img, ids):
    vmem = pl.BlockSpec(memory_space=pltpu.VMEM)
    hbm = pl.BlockSpec(memory_space=pl.ANY)
    f32, bf16 = jnp.float32, jnp.bfloat16
    dma = pltpu.SemaphoreType.DMA
    return pl.pallas_call(
        main_kernel,
        in_specs=[pl.BlockSpec(memory_space=pltpu.SMEM)] + [hbm] * 4 + [vmem] * 2,
        out_specs=[vmem] * 3 + [hbm] * 2,
        out_shape=[jax.ShapeDtypeStruct((DIM, DIM), f32)] * 2 + [jax.ShapeDtypeStruct((3, 8, 128), f32)]
        + [jax.ShapeDtypeStruct((2, SLOTS, ROWS, DIM), bf16), jax.ShapeDtypeStruct((ROWS, DIM), f32)],
        scratch_shapes=[
            pltpu.VMEM((ROWS, DIM), bf16), pltpu.VMEM((ROWS, DIM), bf16),
            pltpu.VMEM((DIM, DIM), bf16), pltpu.VMEM((DIM, DIM), f32),
            pltpu.VMEM((ROWS, DIM), f32), pltpu.VMEM((ROWS, 1), f32), pltpu.VMEM((ROWS, 1), f32),
            pltpu.VMEM((ROWS, DIM), bf16), pltpu.VMEM((ROWS, DIM), bf16),
            pltpu.VMEM((ROWS, DIM), f32), pltpu.VMEM((ROWS, DIM), f32),
            pltpu.VMEM((4, TILE, DIM), bf16),
            pltpu.VMEM((ROWS, TILE), f32), pltpu.VMEM((ROWS, TILE), f32),
            pltpu.VMEM((ROWS, TILE), bf16), pltpu.VMEM((ROWS, TILE), bf16),
            pltpu.VMEM((SLOTS, 1, ROWS), jnp.int32), pltpu.VMEM((1, TILE), jnp.int32),
            pltpu.VMEM((SLOTS, 3, 8, 128), f32), pltpu.VMEM((HALF_DIM, DIM), f32),
            pltpu.VMEM((3, RS_ROWS[0], COLOR), f32), pltpu.VMEM((3, RS_ROWS[1], COLOR), f32),
            pltpu.VMEM((3, RS_ROWS[2], COLOR), f32),
            dma((2, 2, 3, 7)), dma((2, 2, 3, 7)), dma((2, 2, 8)), dma((2, 2, 8)), dma((SLOTS,)), dma((SLOTS,)),
            dma((4,)), dma((2, 2)), dma((2,)), dma((2, 2)), dma((SLOTS,)), dma((SLOTS,)),
            dma((2, 2)), dma((2, 2)), dma((2, 3, 6)), dma((2, 3, 6)),
        ],
        compiler_params=pltpu.CompilerParams(collective_id=0, has_side_effects=True, vmem_limit_bytes=67043328),
    )(scal, feat_txt, feat_img, w_txt, w_img, ids[:, None], ids[None, :])


def solution(mesh):
    n_dev = mesh.shape["data"]

    def local_fn(feat_img, feat_txt, w_img, w_txt, log_temp, logit_bias, pair_ids):
        total_rows = feat_img.shape[0] * n_dev
        temp_scale = jnp.exp(log_temp)
        scal = jnp.stack([-temp_scale * LOG2E, -logit_bias * LOG2E, temp_scale / total_rows])
        dw_img, dw_txt, totals = main_call(scal, feat_txt, feat_img, w_txt, w_img, pair_ids)[:3]
        sums = jnp.sum(totals, axis=(1, 2))
        return (sums[0] / (LOG2E * total_rows), temp_scale * sums[1] / total_rows, sums[2] / total_rows, dw_img, dw_txt)

    return jax.shard_map(
        local_fn,
        mesh=mesh,
        in_specs=(P("data", None), P("data", None), P(None, None), P(None, None), P(), P(), P("data")),
        out_specs=(P(), P(), P(), P(None, None), P(None, None)),
        check_vma=False,
    )
```

time: 495 us -> 399 us (0.81)
  Pallas kernels: 281 us -> 372 us
  waiting for transfers between devices: 90.4 us -> 0 us
  blocking collectives: 31.6 us -> 0 us
  matrix products: 25.2 us -> 0 us
  other arithmetic: 17.8 us -> 1.4 us
  between operations: 21.3 us -> 7.77 us
  local copies, waits for them, and re-layouts: 20.1 us -> 10.1 us
    pallas_call x1, Pallas kernels: 281 us -> 372 us  [main_call(): pl.pallas_call(main_kernel, in_specs=[pl.BlockSpec(memory_space=pltpu.SME...]
    psum x1 -> x0, waiting for transfers between devices: 90.4 us -> none  [local_fn(): sums, dw_img, dw_txt = lax.psum((sums, dw_img, dw_txt), 'data')]
    psum x1 -> x0, blocking collectives: 31.6 us -> none  [local_fn(): sums, dw_img, dw_txt = lax.psum((sums, dw_img, dw_txt), 'data')]
    dot_general x4 -> x0, matrix products: 25.2 us -> none  [the longest x2 12.7 us: embed_rows(): raw_emb = jnp.dot(feat_rows, weights, preferred_element_type=jnp.float32)]
    unnamed x36 -> x4, local copies, waits for them, and re-layouts: 18.4 us -> 7.76 us
    reduce_sum x4 -> x1, other arithmetic: 9.22 us -> 0.81 us  [local_fn(): sums = jnp.sum(totals, axis=(1, 2))]
    convert_element_type x2 -> x0, other arithmetic: 5.94 us -> none  [embed_rows(): return (unit_emb, inv_norm, unit_emb.astype(jnp.bfloat16))]
  transfers between devices with their start and end apart: 1 -> 0, of which waited for: 1 -> 0; matrix products, arithmetic and copies ran while one was open for 1% -> 0% of each run, Pallas kernels for 0% -> 0%
where the time goes in v3:
time: 399 us; the launch traced here: 392 us
  Pallas kernels  372 us (93%)
  local copies, waits for them, and re-layouts  10.1 us (3%)
  between operations  7.77 us (2%)
    pallas_call x1, Pallas kernels, main_call(): pl.pallas_call(main_kernel, in_specs=[pl.BlockSpec(memory_space=pltpu.SME...  372 us

profile of v3, /device:TPU:0, one launch (start us, length us, event | category | flops | bytes accessed | tf_op | source)
XLA Modules:
  0.0 391.7 jit_solution(8870059619136618620)
XLA Ops:
  2.0 0.6 pad_maximum_fusion.scal
  2.6 1.7 copy.12.ids_own
  4.3 372.5 %shard_map.110 = (f32[1152,1152]{1,0:T(8,128)}, f32[1152,1152]{1,0:T(8,128)}, f32[3,8,128]{2,1,0:T(8,128)}, bf16[2,16,1024,1152]{3,2,1,0:T(8,128)(2,1)}, f32[1024,1152]{1,0:T(8,128)}) custom-call(f32[3]{0:T(128)} %pad_maximum_fusion.scal, bf16[1024,1152]{1,0:T(8,128)(2,1)} %feat_txt.1, bf16[1024,1152]{1,0:T(8,128)(2,1)} %feat_img.1, ...), custom_call_target="tpu_custom_call" | custom-call | tf_op jit(solution)/shard_map/pallas_call | solution.py:426
  376.7 0.8 reduce_sum.9
  377.5 0.6 fusion
  380.1 0.0 copy-start
  380.1 5.4 %copy.17 = f32[1152,1152]{1,0:T(8,128)} copy(f32[1152,1152]{1,0:T(8,128)} %get-tuple-element.22) | data formatting | bytes 10616832
  385.5 0.0 copy-done
  385.5 2.4 copy.18
Async XLA Ops:
  380.1 5.4 %copy-start = (f32[1152,1152]{1,0:T(8,128)S(1)}, f32[1152,1152]{1,0:T(8,128)}, u32[]{:S(2)}) copy-start(f32[1152,1152]{1,0:T(8,128)} %get-tuple-element.23) | copy-start | bytes 15925252

commit v4 on v3

--- a/solution.py
+++ b/solution.py
@@ -17,12 +17,12 @@
 COLOR = DIM // 3
 LINK_BITS = (2, 4, 8)
 SLOTS = 16
-ROW_PIECE = 32
-D1_PIECE = (512, 256)
+ROW_PIECE = 128
+D1_PIECE = (256, 512)
 D2_PIECE = (512, 512)
 HALF_DIM = DIM // 2
 RS_ROWS = (HALF_DIM // 2, HALF_DIM // 4, HALF_DIM // 8)
-REDUCE_STEPS = {50: 1, 53: 2, 55: 3, 57: 4, 59: 5, 61: 6, 64: 7}
+REDUCE_STEPS = {54: 1, 57: 2, 59: 3, 60: 4, 61: 5, 62: 6, 64: 7}
 
 
 def transfer_table(color):
@@ -71,22 +71,16 @@
             for m in range(0, ROWS, D2_PIECE[0]) for n in range(0, DIM, D2_PIECE[1])]
 
 
-def fold_cols(x):
-    y = x[:, 0:128]
-    for c in range(1, TILE // 128):
-        y = y + x[:, c * 128:(c + 1) * 128]
-    return y
-
-
 def vpu_pieces(want, neg_scale, neg_bias, sim, grad_out, ids_own, ids_rem, sums):
-    state = {}
+    state = {"terms": 0}
 
     def add(name, value):
         state[name] = state[name] + value if name in state else value
 
-    def piece(r0):
-        s = sim[r0:r0 + ROW_PIECE, :]
-        neg_y = jnp.where(ids_own[r0:r0 + ROW_PIECE, :] == ids_rem[...], -1.0, 1.0)
+    def chunk(r0, c0):
+        rows, cols = slice(r0, r0 + ROW_PIECE), slice(c0, c0 + 128)
+        s = sim[rows, cols]
+        neg_y = jnp.where(ids_own[rows, :] == ids_rem[:, cols], -1.0, 1.0)
         yz = (s * neg_scale + neg_bias) * neg_y
         if want:
             e = jnp.exp2(-jnp.abs(yz))
@@ -94,28 +88,42 @@
             grad = jnp.where(yz <= 0, r, e * r) * neg_y
             low = jnp.minimum(yz, 0.0)
             gs = grad * s
-            for i in range(0, ROW_PIECE, 8):
-                e_i = e[i:i + 8]
-                state["prod"] = state["prod"] + (e_i + state["prod"] * e_i) if "prod" in state else e_i
-                add("low", low[i:i + 8])
-                add("gs", gs[i:i + 8])
-                add("g", grad[i:i + 8])
-            if (r0 + ROW_PIECE) % 512 == 0:
+            while e.shape[0] > 8:
+                mid = e.shape[0] // 2
+                e = e[:mid] + (e[mid:] + e[:mid] * e[mid:])
+            state["prod"] = state["prod"] + (e + state["prod"] * e) if "prod" in state else e
+            state["terms"] += ROW_PIECE // 8
+            add("low", jnp.sum(low.reshape(-1, 8, 128), axis=0))
+            add("gs", jnp.sum(gs.reshape(-1, 8, 128), axis=0))
+            add("g", jnp.sum(grad.reshape(-1, 8, 128), axis=0))
+            if state["terms"] == 64:
                 state["low"] = state["low"] - jnp.log1p(state.pop("prod")) * LOG2E
-            if r0 + ROW_PIECE == ROWS:
-                sums[0][...] -= fold_cols(state["low"])
-                sums[1][...] += fold_cols(state["gs"])
-                sums[2][...] += fold_cols(state["g"])
+                state["terms"] = 0
         else:
             grad = neg_y / (1.0 + jnp.exp2(yz))
-        grad_out[r0:r0 + ROW_PIECE, :] = grad.astype(jnp.bfloat16)
+        grad_out[rows, cols] = grad.astype(jnp.bfloat16)
+
+    def piece(r0):
+        for c0 in range(0, TILE, 128):
+            chunk(r0, c0)
+        if want and r0 + ROW_PIECE == ROWS:
+            sums[0][...] -= state["low"]
+            sums[1][...] += state["gs"]
+            sums[2][...] += state["g"]
 
     return [functools.partial(piece, r0) for r0 in range(0, ROWS, ROW_PIECE)]
 
 
-def main_kernel(scal, feat_txt, feat_img, w_txt, w_img, ids_own, ids_row,
+def ids_column(row):
+    shape = (128, 128)
+    diagonal = lax.broadcasted_iota(jnp.int32, shape, 0) == lax.broadcasted_iota(jnp.int32, shape, 1)
+    picked = jnp.where(diagonal, jnp.broadcast_to(row.astype(jnp.float32), shape), 0.0)
+    return jnp.broadcast_to(jnp.sum(picked, axis=1, keepdims=True), shape).astype(jnp.int32)
+
+
+def main_kernel(scal, feat_txt, feat_img, w_txt, w_img, ids_row,
                 dw_img, dw_txt, totals, gat, unit_hbm,
-                feat0, feat1, wgt, part, unit, inv0, inv1, emb_txt, emb_img, acc_img, acc_txt,
+                ids_own, feat0, feat1, wgt, part, unit, inv0, inv1, emb_txt, emb_img, acc_img, acc_txt,
                 tiles, sim0, sim1, grad0, grad1, ids_all, ids_cur, sums_all, rx_pair, rx1, rx2, rx3,
                 send_sem, recv_sem, pair_send, pair_recv, ids_send, ids_recv, tile_sem, load_sem, unit_sem, own_sem,
                 sum_send, sum_recv, half_send, half_recv, ring_send, ring_recv):
@@ -347,6 +355,8 @@
     send_own(0, 1)
     unit_out = pltpu.make_async_copy(unit, unit_hbm, unit_sem.at[0])
     unit_out.start()
+    for block in range(0, ROWS, 128):
+        ids_own[block:block + 128, :] = ids_column(ids_row[:, block:block + 128])
     acc_img[...] = jnp.zeros_like(acc_img)
     acc_txt[...] = jnp.zeros_like(acc_txt)
     for out in sums:
@@ -425,11 +435,12 @@
     dma = pltpu.SemaphoreType.DMA
     return pl.pallas_call(
         main_kernel,
-        in_specs=[pl.BlockSpec(memory_space=pltpu.SMEM)] + [hbm] * 4 + [vmem] * 2,
+        in_specs=[pl.BlockSpec(memory_space=pltpu.SMEM)] + [hbm] * 4 + [vmem],
         out_specs=[vmem] * 3 + [hbm] * 2,
         out_shape=[jax.ShapeDtypeStruct((DIM, DIM), f32)] * 2 + [jax.ShapeDtypeStruct((3, 8, 128), f32)]
         + [jax.ShapeDtypeStruct((2, SLOTS, ROWS, DIM), bf16), jax.ShapeDtypeStruct((ROWS, DIM), f32)],
         scratch_shapes=[
+            pltpu.VMEM((ROWS, 128), jnp.int32),
             pltpu.VMEM((ROWS, DIM), bf16), pltpu.VMEM((ROWS, DIM), bf16),
             pltpu.VMEM((DIM, DIM), bf16), pltpu.VMEM((DIM, DIM), f32),
             pltpu.VMEM((ROWS, DIM), f32), pltpu.VMEM((ROWS, 1), f32), pltpu.VMEM((ROWS, 1), f32),
@@ -447,7 +458,7 @@
             dma((2, 2)), dma((2, 2)), dma((2, 3, 6)), dma((2, 3, 6)),
         ],
         compiler_params=pltpu.CompilerParams(collective_id=0, has_side_effects=True, vmem_limit_bytes=67043328),
-    )(scal, feat_txt, feat_img, w_txt, w_img, ids[:, None], ids[None, :])
+    )(scal, feat_txt, feat_img, w_txt, w_img, ids[None, :])
 
 
 def solution(mesh):

time: 399 us -> 383 us (0.960)
  Pallas kernels: 372 us -> 358 us
    pallas_call x1, Pallas kernels: 372 us -> 358 us  [main_call(): pl.pallas_call(main_kernel, in_specs=[pl.BlockSpec(memory_space=pltpu.SME...]
where the time goes in v4:
time: 383 us; the launch traced here: 376 us
  Pallas kernels  358 us (93%)
  local copies, waits for them, and re-layouts  8.35 us (2%)
  between operations  7.77 us (2%)
    pallas_call x1, Pallas kernels, main_call(): pl.pallas_call(main_kernel, in_specs=[pl.BlockSpec(memory_space=pltpu.SME...  358 us
    unnamed x4, local copies, waits for them, and re-layouts  7.76 us

profile of v4, /device:TPU:0, one launch (start us, length us, event | category | flops | bytes accessed | tf_op | source)
XLA Modules:
  0.0 375.6 jit_solution(5407539639435593431)
XLA Ops:
  2.0 0.6 pad_maximum_fusion.scal
  2.6 358.1 %shard_map.110 = (f32[1152,1152]{1,0:T(8,128)}, f32[1152,1152]{1,0:T(8,128)}, f32[3,8,128]{2,1,0:T(8,128)}, bf16[2,16,1024,1152]{3,2,1,0:T(8,128)(2,1)}, f32[1024,1152]{1,0:T(8,128)}) custom-call(f32[3]{0:T(128)} %pad_maximum_fusion.scal, bf16[1024,1152]{1,0:T(8,128)(2,1)} %feat_txt.1, bf16[1024,1152]{1,0:T(8,128)(2,1)} %feat_img.1, ...), custom_call_target="tpu_custom_call" | custom-call | tf_op jit(solution)/shard_map/pallas_call | solution.py:436
  360.7 0.8 reduce_sum.9
  361.5 0.6 fusion
  364.0 0.0 copy-start
  364.0 5.4 %copy.16 = f32[1152,1152]{1,0:T(8,128)} copy(f32[1152,1152]{1,0:T(8,128)} %get-tuple-element.22) | data formatting | bytes 10616832
  369.4 0.0 copy-done
  369.4 2.4 copy.17
Async XLA Ops:
  364.0 5.4 %copy-start = (f32[1152,1152]{1,0:T(8,128)S(1)}, f32[1152,1152]{1,0:T(8,128)}, u32[]{:S(2)}) copy-start(f32[1152,1152]{1,0:T(8,128)} %get-tuple-element.23) | copy-start | bytes 15925252

commit v5 on v4

--- a/solution.py
+++ b/solution.py
@@ -151,7 +151,7 @@
                                             device_id=(dev,), device_id_type=MESH_ID)
 
     def rows_of(half):
-        return pl.ds(half * TILE, TILE)
+        return pl.ds(half * TILE if isinstance(half, int) else pl.multiple_of(half * TILE, TILE), TILE)
 
     def transfer(arr, half, color, i):
         link, slot = transfer_table(color)[i]
@@ -364,8 +364,11 @@
     load(1, 0).wait()
     load(1, 1).wait()
     unit_out.wait()
-    for half in range(2):
+
+    @pl.loop(0, 2)
+    def _(half):
         embed_half(1, half)
+
     for half in range(2):
         own_copy(1, half).wait()
 

time: 383 us -> 376 us (0.982); the launches traced: 376 us -> 375 us
  no operation moved by 1% of the time
where the time goes in v5:
time: 376 us; the launch traced here: 375 us
  Pallas kernels  358 us (95%)
  local copies, waits for them, and re-layouts  8.35 us (2%)
  between operations  7.33 us (2%)
    pallas_call x1, Pallas kernels, main_call(): pl.pallas_call(main_kernel, in_specs=[pl.BlockSpec(memory_space=pltpu.SME...  358 us
    unnamed x4, local copies, waits for them, and re-layouts  7.76 us

profile of v5, /device:TPU:0, one launch (start us, length us, event | category | flops | bytes accessed | tf_op | source)
XLA Modules:
  0.0 375.2 jit_solution(17880288075954978655)
XLA Ops:
  2.0 0.6 pad_maximum_fusion.scal
  2.6 358.1 %shard_map.110 = (f32[1152,1152]{1,0:T(8,128)}, f32[1152,1152]{1,0:T(8,128)}, f32[3,8,128]{2,1,0:T(8,128)}, bf16[2,16,1024,1152]{3,2,1,0:T(8,128)(2,1)}, f32[1024,1152]{1,0:T(8,128)}) custom-call(f32[3]{0:T(128)} %pad_maximum_fusion.scal, bf16[1024,1152]{1,0:T(8,128)(2,1)} %feat_txt.1, bf16[1024,1152]{1,0:T(8,128)(2,1)} %feat_img.1, ...), custom_call_target="tpu_custom_call" | custom-call | tf_op jit(solution)/shard_map/pallas_call | solution.py:439
  360.7 0.8 reduce_sum.9
  361.5 0.6 fusion
  364.0 0.0 copy-start
  364.0 5.4 %copy.16 = f32[1152,1152]{1,0:T(8,128)} copy(f32[1152,1152]{1,0:T(8,128)} %get-tuple-element.22) | data formatting | bytes 10616832
  369.4 0.0 copy-done
  369.4 2.4 copy.17
Async XLA Ops:
  364.0 5.4 %copy-start = (f32[1152,1152]{1,0:T(8,128)S(1)}, f32[1152,1152]{1,0:T(8,128)}, u32[]{:S(2)}) copy-start(f32[1152,1152]{1,0:T(8,128)} %get-tuple-element.23) | copy-start | bytes 15925252

commit v6 on v5

--- a/solution.py
+++ b/solution.py
@@ -385,8 +385,12 @@
             base = (start // 2) % 2
             buf = 2 * lax.rem(it + base, 2)
             for par in range(2):
-                for k in range(n_iter):
-                    pl.when(it == k)(functools.partial(comm, start + 2 * k + par))
+                for first in range(0, n_iter, 4):
+                    @pl.when(lax.div(it, 4) == first // 4)
+                    def _():
+                        for k in range(first, min(first + 4, n_iter)):
+                            pl.when(it == k)(functools.partial(comm, start + 2 * k + par))
+
                 step(par, arr, arr, arr, buf + par, (2 - buf) + par)
 
     run_loop(0, 2)

time: 376 us -> 376 us (level)
  no operation moved by 1% of the time
where the time goes in v6:
time: 376 us; the launch traced here: 375 us
  Pallas kernels  358 us (95%)
  local copies, waits for them, and re-layouts  8.35 us (2%)
  between operations  7.33 us (2%)
    pallas_call x1, Pallas kernels, main_call(): pl.pallas_call(main_kernel, in_specs=[pl.BlockSpec(memory_space=pltpu.SME...  358 us
    unnamed x4, local copies, waits for them, and re-layouts  7.76 us

profile of v6, /device:TPU:0, one launch (start us, length us, event | category | flops | bytes accessed | tf_op | source)
XLA Modules:
  0.0 375.2 jit_solution(8050410916741762617)
XLA Ops:
  2.0 0.6 pad_maximum_fusion.scal
  2.6 358.2 %shard_map.110 = (f32[1152,1152]{1,0:T(8,128)}, f32[1152,1152]{1,0:T(8,128)}, f32[3,8,128]{2,1,0:T(8,128)}, bf16[2,16,1024,1152]{3,2,1,0:T(8,128)(2,1)}, f32[1024,1152]{1,0:T(8,128)}) custom-call(f32[3]{0:T(128)} %pad_maximum_fusion.scal, bf16[1024,1152]{1,0:T(8,128)(2,1)} %feat_txt.1, bf16[1024,1152]{1,0:T(8,128)(2,1)} %feat_img.1, ...), custom_call_target="tpu_custom_call" | custom-call | tf_op jit(solution)/shard_map/pallas_call | solution.py:443
  360.7 0.8 reduce_sum.9
  361.5 0.6 fusion
  364.1 0.0 copy-start
  364.1 5.4 %copy.16 = f32[1152,1152]{1,0:T(8,128)} copy(f32[1152,1152]{1,0:T(8,128)} %get-tuple-element.22) | data formatting | bytes 10616832
  369.5 0.0 copy-done
  369.5 2.4 copy.17
Async XLA Ops:
  364.1 5.4 %copy-start = (f32[1152,1152]{1,0:T(8,128)S(1)}, f32[1152,1152]{1,0:T(8,128)}, u32[]{:S(2)}) copy-start(f32[1152,1152]{1,0:T(8,128)} %get-tuple-element.23) | copy-start | bytes 15925252
